TPU v7x, 32 devices: a whole 2x2x4 slice. The times are simulated.
32 devices in a mesh: gz: 2 (over y), row: 4 (over z), col: 4 (over x, core).
Axes of the slice: x: 2, y: 2, z: 4, core: 2. Of those that a mesh axis runs over, the one named last changes fastest.
Arguments:
- lpanel: bfloat16 [2, 2, 1024, 2048], P(None, 'gz', 'row', 'col'), may hold values from -6 to 6
- upanel: bfloat16 [2, 2, 2048, 4096], P(None, 'gz', 'row', 'col'), may hold values from -0.125 to 0.125
- rowmap: int32 [2, 2, 4], P(None, 'gz', 'row'), may hold values from 0 to 1
- colmap: int32 [2, 2, 16], P(None, 'gz', 'col'), may hold values from 0 to 1
- blockmask: int32 [2, 2, 4, 16], P(None, 'gz', 'row', 'col'), may hold values 0 or 1
- front_blocks: bfloat16 [2, 2048, 2048], P(None, 'row', ('gz', 'col')), may hold values from -6 to 6
Outputs:
- front_update: bfloat16 [2, 2048, 2048], P(None, 'row', ('gz', 'col'))
All inputs are finite; a program needn't handle non-finite values. No bound on the sum of `blockmask` on one device may be relied on, other than what follows from the above.
Results may differ from a plain program's by a relative error of at most 0.008.
Values may be sent and summed in bfloat16 or wider, within the bound.
A program may use at most 64 MiB of HBM per device.

v0:
```python
import functools

import jax
import jax.numpy as jnp
from jax import lax
from jax.experimental import pallas as pl
from jax.experimental.pallas import tpu as pltpu
from jax.sharding import PartitionSpec as P

CB = 4
FRB = 2
MESH = pl.DeviceIdType.MESH


def column_sums(schur, cols_of, live, layers):
    width = schur.shape[0]
    blocks = schur.reshape(width, CB, width)
    targets = cols_of[:, None] == jnp.arange(layers, dtype=jnp.int32)[None, :]
    col_select = targets.astype(jnp.float32) * live.astype(jnp.float32)[:, None]
    return jnp.einsum("bjk,jl->lbk", blocks, col_select, precision=lax.Precision.HIGHEST)


def general(lpanel, upanel, rowmap, colmap, blockmask, front_blocks):
    layers = lax.axis_size("gz")
    width = lpanel.shape[2]
    levels = lpanel.shape[0]
    tiles = []
    for depth in range(levels):
        left_rows = lax.all_gather(lpanel[depth, 0], "col", axis=1, tiled=True)
        tiles.append(
            jnp.dot(
                left_rows,
                lax.all_gather(upanel[depth, 0], "row", axis=0, tiled=True),
                preferred_element_type=jnp.float32,
            )
        )
    results = []
    every_row = lax.all_gather(rowmap[:, :, 0], "gz", axis=1, tiled=True)
    for depth in range(levels):
        sums = column_sums(tiles[depth], colmap[depth, 0], blockmask[depth, 0, 0], layers).astype(
            jnp.bfloat16
        )
        arrived = lax.all_to_all(sums, "gz", split_axis=0, concat_axis=0, tiled=True)
        row_select = (
            every_row[depth][:, None] == jnp.arange(FRB, dtype=jnp.int32)[None, :]
        ).astype(jnp.float32)
        placed = jnp.einsum(
            "sf,sbk->fbk", row_select, arrived.astype(jnp.float32), precision=lax.Precision.HIGHEST
        )
        placed = placed.reshape(FRB * width, width)
        results.append((front_blocks[depth].astype(jnp.float32) - placed).astype(jnp.bfloat16))
    return jnp.stack(results)


def kernel(
    rows, cols, layers, levels, width,
    l_hbm, u_hbm, cm_ref, live_ref, rm_ref, front_hbm, out_ref,
    l_ref, u_ref, front_ref, crossed, l_all, live_all, own, part, p_in, y_out, y_in, rm_in,
    in_sem, x_send, x_recv, l_send, l_recv, loc_sem, post_send, relay_send, m_send, m_recv, m_loc,
    p_send, p_recv, y_send, y_recv, rm_send, rm_recv,
):
    z = lax.axis_index("row")
    c = lax.axis_index("col")
    g = lax.axis_index("gz")
    far = lax.rem(c + cols // 2, cols)
    mate = c + 1 - 2 * lax.rem(c, 2)
    other = 1 - g
    gate = lax.rem(c, 2) == lax.rem(z, 2)

    loads = [pltpu.make_async_copy(u_hbm.at[v], u_ref.at[v], in_sem.at[v]) for v in range(levels)]
    loads.append(pltpu.make_async_copy(front_hbm, front_ref, in_sem.at[levels]))
    first = pltpu.make_async_copy(l_hbm, l_ref, in_sem.at[levels + 1])
    first.start()
    for load in loads:
        load.start()

    barrier = pltpu.get_barrier_semaphore()
    for step in range(1, rows):
        pl.semaphore_signal(
            barrier, inc=1, device_id={"row": lax.rem(z + step, rows)}, device_id_type=MESH
        )
    pl.semaphore_signal(barrier, inc=1, device_id={"col": far}, device_id_type=MESH)
    pl.semaphore_signal(barrier, inc=1, device_id={"col": mate}, device_id_type=MESH)
    pl.semaphore_signal(barrier, inc=1, device_id={"gz": other}, device_id_type=MESH)
    pl.semaphore_wait(barrier, rows + 2)

    def remote(src, dst, send, recv, where):
        return pltpu.make_async_remote_copy(
            src_ref=src, dst_ref=dst, send_sem=send, recv_sem=recv,
            device_id=where, device_id_type=MESH,
        )

    half = width // 2
    pieces = [slice(h * half, (h + 1) * half) for h in range(2)]

    across = [
        remote(l_ref.at[v, pieces[1]], crossed.at[v], x_send.at[v], x_recv.at[v], {"col": far})
        for v in range(levels)
    ]

    def place(v, h):
        to = c if h == 0 else far
        block = l_ref.at[v, pieces[0]] if h == 0 else crossed.at[v]
        spot = l_all.at[v, z, pieces[h]]
        copy = remote(block, spot, l_send.at[v, h], l_recv.at[v, h, z], {"row": to})
        return to, copy, block, spot

    def start_place(v, h):
        to, copy, block, spot = place(v, h)

        @pl.when(to != z)
        def _():
            copy.start()

        @pl.when(to == z)
        def _():
            pltpu.make_async_copy(block, spot, loc_sem.at[v, h]).start()

    first.wait()
    for v in range(levels):
        across[v].start()
    for v in range(levels):
        start_place(v, 0)

    own_live = pltpu.make_async_copy(live_ref, live_all.at[z], m_loc)
    own_live.start()
    live_out = []
    for step in range(1, rows):
        to = lax.rem(z + step, rows)
        live_out.append(
            remote(live_ref, live_all.at[z], m_send.at[step], m_recv.at[z], {"row": to})
        )
        live_out[-1].start()
    rm_copy = remote(rm_ref, rm_in, rm_send, rm_recv, {"gz": other})
    rm_copy.start()

    across[0].wait_recv()
    start_place(0, 1)

    own_live.wait()
    for step in range(1, rows):
        src = lax.rem(z + step, rows)
        remote(live_ref, live_all.at[src], m_send.at[step], m_recv.at[src], {"row": src}).wait_recv()

    low = 1 - z // (rows // 2)

    def order(i):
        near = jnp.int32(i) if isinstance(i, int) else i
        wrap = near // (rows // 2)
        up = rows - 1 - near + wrap * (2 * near - rows - rows // 2 + 1)
        return low * up + (1 - low) * (rows - 1 - up)

    def hop(v, a, l, side, to):
        return remote(
            part.at[v, a, l], p_in.at[v, side, a, l],
            p_send.at[v, a, l], p_recv.at[v, side, a, l], {"row": to},
        )

    turns = (other, g)
    right, left = lax.rem(z + 1, rows), lax.rem(z + rows - 1, rows)

    def send(v, a, l, side, to):
        part[v, a, l] = own[v, a, l].astype(jnp.bfloat16)
        hop(v, a, l, side, to).start()

    def passes(v, a, h):
        spot = l_all.at[v, a, pieces[h]]
        post = remote(spot, spot, post_send.at[v, a], l_recv.at[v, h, a], {"col": far})
        relay = remote(spot, spot, relay_send.at[v, h, a], l_recv.at[v, h, a], {"col": mate})
        return post, relay

    def gather_half(v, a, h):
        post, relay = passes(v, a, h)

        @pl.when(a == z)
        def _():
            spot = l_all.at[v, z, pieces[h]]
            pltpu.make_async_copy(l_ref.at[v, pieces[h]], spot, loc_sem.at[v, h]).wait()

        @pl.when(a != z)
        def _():
            relay.wait_recv()

        post.start()
        relay.start()

    def take_half(v, a, h):
        _post, relay = passes(v, a, h)
        relay.wait_recv()
        relay.start()

    def gather(v, i):
        a = order(i)
        pl.when(c == z)(lambda: gather_half(v, a, 0))
        pl.when(far == z)(lambda: gather_half(v, a, 1))

    def take(v, i):
        a = order(i)
        pl.when(c == z)(lambda: take_half(v, a, 1))
        pl.when(far == z)(lambda: take_half(v, a, 0))

    def item(v, i):
        a = order(i)

        @pl.when(i == 0)
        def _():
            take(v, i)

        @pl.when(i < rows - 1)
        def _():
            take(v, i + 1)

        @pl.when(jnp.logical_not(gate))
        def _():
            for h in range(2):
                passes(v, a, h)[1].wait_recv()

        block = l_all[v, a]
        for j in range(CB):
            t = jnp.dot(
                block, u_ref[v, :, j * width : (j + 1) * width], preferred_element_type=jnp.float32
            )
            to_layer = cm_ref[v : v + 1, j : j + 1]
            live = live_all[a, v : v + 1, j : j + 1]
            for l in range(layers):
                m = jnp.where(to_layer == l, live, 0).astype(jnp.float32)
                if j == 0:
                    own[v, a, l] = t * m
                else:
                    own[v, a, l] += t * m

        @pl.when(jnp.logical_and(a > z, z == 0))
        def _():
            for l in turns:
                send(v, a, l, 0, right)

        @pl.when(jnp.logical_and(a < z, z == rows - 1))
        def _():
            for l in turns:
                send(v, a, l, 1, left)

        if v + 1 < levels:
            gather(v + 1, i)

    def collect(v, a, l, side):
        hop(v, a, l, side, right).wait_recv()
        own[v, a, l] += p_in[v, side, a, l].astype(jnp.float32)

    def forward(v, i):
        a = order(i)

        @pl.when(jnp.logical_and(a > z, z > 0))
        def _():
            for l in turns:
                collect(v, a, l, 0)
                send(v, a, l, 0, right)

        @pl.when(jnp.logical_and(a < z, z < rows - 1))
        def _():
            for l in turns:
                collect(v, a, l, 1)
                send(v, a, l, 1, left)

    def finish(v, l):
        @pl.when(z > 0)
        def _():
            collect(v, z, l, 0)

        @pl.when(z < rows - 1)
        def _():
            collect(v, z, l, 1)

    def over_rows(step, v):
        def body(i, carry):
            step(v, i)
            return carry

        lax.fori_loop(0, rows, body, 0)

    for v in range(levels):
        if v == 0:
            over_rows(gather, v)
        if v + 1 < levels:
            across[v + 1].wait_recv()
            start_place(v + 1, 1)
        loads[v].wait()
        over_rows(item, v)

    ways = []
    for v in range(levels):
        over_rows(forward, v)

        finish(v, other)
        y_out[v] = own[v, z, other].astype(jnp.bfloat16)
        way = remote(y_out.at[v], y_in.at[v], y_send.at[v], y_recv.at[v], {"gz": other})
        way.start()
        ways.append(way)
        finish(v, g)

    loads[levels].wait()
    rm_copy.wait()
    for v in range(levels):
        mine = own[v, z, g].astype(jnp.bfloat16).astype(jnp.float32)
        ways[v].wait_recv()
        theirs = y_in[v].astype(jnp.float32)
        for f in range(FRB):
            lines = slice(f * width, (f + 1) * width)
            here = (rm_ref[v : v + 1, :] == f).astype(jnp.float32)
            away = (rm_in[v : v + 1, :] == f).astype(jnp.float32)
            total = here * mine + away * theirs
            out_ref[v, lines, :] = (front_ref[v, lines, :].astype(jnp.float32) - total).astype(
                out_ref.dtype
            )

    for copy in live_out:
        copy.wait_send()
    for v in range(levels):
        across[v].wait_send()
        ways[v].wait_send()
        for h in range(2):
            to, copy, _block, _spot = place(v, h)
            pl.when(to != z)(copy.wait_send)
        for a in range(rows):
            for h in range(2):
                post, relay = passes(v, a, h)
                pl.when(gate)(relay.wait_send)
                if h == 0:
                    pl.when(gate)(post.wait_send)
            for l in range(layers):
                pl.when(a != z)(hop(v, a, l, 0, right).wait_send)


def stationary(rows, cols, layers, lpanel, upanel, rowmap, colmap, blockmask, front_blocks):
    levels, _, width, depth = lpanel.shape
    bf16 = jnp.bfloat16
    vmem = pl.BlockSpec(memory_space=pltpu.VMEM)
    hbm = pl.BlockSpec(memory_space=pl.ANY)
    dma = pltpu.SemaphoreType.DMA
    return pl.pallas_call(
        functools.partial(kernel, rows, cols, layers, levels, width),
        out_shape=jax.ShapeDtypeStruct(front_blocks.shape, front_blocks.dtype),
        in_specs=[hbm, hbm, vmem, vmem, vmem, hbm],
        out_specs=vmem,
        scratch_shapes=[
            pltpu.VMEM((levels, width, depth), bf16),
            pltpu.VMEM(upanel[:, 0].shape, bf16),
            pltpu.VMEM(front_blocks.shape, bf16),
            pltpu.VMEM((levels, width // 2, depth), bf16),
            pltpu.VMEM((levels, rows, width, depth), bf16),
            pltpu.VMEM((rows, levels, CB), jnp.int32),
            pltpu.VMEM((levels, rows, layers, width, width), jnp.float32),
            pltpu.VMEM((levels, rows, layers, width, width), bf16),
            pltpu.VMEM((levels, 2, rows, layers, width, width), bf16),
            pltpu.VMEM((levels, width, width), bf16),
            pltpu.VMEM((levels, width, width), bf16),
            pltpu.VMEM((levels, 1), jnp.int32),
            dma((levels + 2,)),
            dma((levels,)),
            dma((levels,)),
            dma((levels, 2)),
            dma((levels, 2, rows)),
            dma((levels, 2)),
            dma((levels, rows)),
            dma((levels, 2, rows)),
            dma((rows,)),
            dma((rows,)),
            dma,
            dma((levels, rows, layers)),
            dma((levels, 2, rows, layers)),
            dma((levels,)),
            dma((levels,)),
            dma,
            dma,
        ],
        compiler_params=pltpu.CompilerParams(collective_id=0, has_side_effects=True),
    )(
        lpanel[:, 0], upanel[:, 0], colmap[:, 0], blockmask[:, 0, 0], rowmap[:, 0], front_blocks
    )


def solution(mesh):
    rows, cols, layers = mesh.shape["row"], mesh.shape["col"], mesh.shape["gz"]
    body = general
    if rows == cols == 2 * layers and layers == 2:
        body = functools.partial(stationary, rows, cols, layers)
    return jax.shard_map(
        body,
        mesh=mesh,
        in_specs=(
            P(None, "gz", "row", "col"),
            P(None, "gz", "row", "col"),
            P(None, "gz", "row"),
            P(None, "gz", "col"),
            P(None, "gz", "row", "col"),
            P(None, "row", ("gz", "col")),
        ),
        out_specs=P(None, "row", ("gz", "col")),
        check_vma=False,
    )
```

profile of v0, /device:TPU:0, one launch (start us, length us, event | category | flops | bytes accessed | tf_op | source)
XLA Modules:
  0.0 67.4 jit_solution(9755517779803635400)
XLA Ops:
  0.0 1.3 %copy.7.rm_ref = s32[2,1]{1,0:T(2,128)} copy(s32[2,1]{0,1:T(1,128)} %bitcast.9) | data formatting | bytes 16 | tf_op jit(solution)/shard_map/squeeze | solution.py:377
  1.3 64.3 %shard_map.64 = bf16[2,512,256]{2,1,0:T(8,128)(2,1)} custom-call(bf16[2,256,512]{2,1,0:T(8,128)(2,1)} %bitcast.6, bf16[2,512,1024]{2,1,0:T(8,128)(2,1)} %bitcast.5, s32[2,4]{1,0:T(2,128)} %bitcast.7, s32[2,4]{1,0:T(2,128)} %bitcast.8, s32[2,1]{1,0:T(2,128)} %copy.7.rm_ref, bf16[2,512,256]{2,1,0:T(8,128)(2,1)} %front_hbm.1), custom_call_target="tpu_custom_call" | custom-call | tf_op jit(solution)/shard_map/pallas_call | solution.py:339
  65.6 1.9 %copy.9 = bf16[2,512,256]{2,1,0:T(8,128)(2,1)} copy(bf16[2,512,256]{2,1,0:T(8,128)(2,1)} %shard_map.64) | data formatting | bytes 1048576
where the time goes:
time: 67.6 us; the launch traced here: 67.4 us
  Pallas kernels  64.3 us (95%)
  local copies, waits for them, and re-layouts  3.16 us (5%)
    pallas_call x1, Pallas kernels, stationary(): pl.pallas_call(functools.partial(kernel, rows, cols, layers, levels, widt...  64.3 us
    unnamed x1, local copies, waits for them, and re-layouts  1.87 us

commit v1 on v0

v1 whole, which is shorter than its diff:
```python
import functools

import jax
import jax.numpy as jnp
from jax import lax
from jax.experimental import pallas as pl
from jax.experimental.pallas import tpu as pltpu
from jax.sharding import PartitionSpec as P

CB = 4
FRB = 2
MESH = pl.DeviceIdType.MESH


def column_sums(schur, cols_of, live, layers):
    width = schur.shape[0]
    blocks = schur.reshape(width, CB, width)
    targets = cols_of[:, None] == jnp.arange(layers, dtype=jnp.int32)[None, :]
    col_select = targets.astype(jnp.float32) * live.astype(jnp.float32)[:, None]
    return jnp.einsum("bjk,jl->lbk", blocks, col_select, precision=lax.Precision.HIGHEST)


def general(lpanel, upanel, rowmap, colmap, blockmask, front_blocks):
    layers = lax.axis_size("gz")
    width = lpanel.shape[2]
    levels = lpanel.shape[0]
    tiles = []
    for depth in range(levels):
        left_rows = lax.all_gather(lpanel[depth, 0], "col", axis=1, tiled=True)
        tiles.append(
            jnp.dot(
                left_rows,
                lax.all_gather(upanel[depth, 0], "row", axis=0, tiled=True),
                preferred_element_type=jnp.float32,
            )
        )
    results = []
    every_row = lax.all_gather(rowmap[:, :, 0], "gz", axis=1, tiled=True)
    for depth in range(levels):
        sums = column_sums(tiles[depth], colmap[depth, 0], blockmask[depth, 0, 0], layers).astype(
            jnp.bfloat16
        )
        arrived = lax.all_to_all(sums, "gz", split_axis=0, concat_axis=0, tiled=True)
        row_select = (
            every_row[depth][:, None] == jnp.arange(FRB, dtype=jnp.int32)[None, :]
        ).astype(jnp.float32)
        placed = jnp.einsum(
            "sf,sbk->fbk", row_select, arrived.astype(jnp.float32), precision=lax.Precision.HIGHEST
        )
        placed = placed.reshape(FRB * width, width)
        results.append((front_blocks[depth].astype(jnp.float32) - placed).astype(jnp.bfloat16))
    return jnp.stack(results)


def kernel(
    rows, cols, layers, levels, width,
    l_hbm, u_hbm, cm_ref, live_ref, rm_ref, front_hbm, out_ref,
    l_ref, u_ref, front_ref, crossed, l_all, live_all, own, part, p_in, y_out, y_in, rm_in,
    in_sem, own_sem, x_send, x_recv, c_send, l_send, l_recv, post_send, relay_send,
    m_send, m_recv, m_loc, p_send, p_recv, y_send, y_recv, rm_send, rm_recv,
):
    z = lax.axis_index("row")
    c = lax.axis_index("col")
    g = lax.axis_index("gz")
    far = lax.rem(c + cols // 2, cols)
    mate = c + 1 - 2 * lax.rem(c, 2)
    other = 1 - g
    last = rows - 1
    entry, second = c == z, far == z
    gate = jnp.logical_or(entry, second)
    low = 1 - z // (rows // 2)
    depth = low * z + (1 - low) * (last - z)
    at_end = depth == 0
    inner = jnp.logical_not(at_end)

    def remote(src, dst, send, recv, where):
        return pltpu.make_async_remote_copy(
            src_ref=src, dst_ref=dst, send_sem=send, recv_sem=recv,
            device_id=where, device_id_type=MESH,
        )

    first = pltpu.make_async_copy(l_hbm, l_ref, in_sem.at[0])
    first.start()
    whole_u = pltpu.make_async_copy(u_hbm, u_ref, in_sem.at[1])
    whole_u.start()
    fronts = pltpu.make_async_copy(front_hbm, front_ref, in_sem.at[2])
    fronts.start()

    def own_load(v):
        return pltpu.make_async_copy(l_hbm.at[v], l_all.at[v, z], own_sem.at[v])

    @pl.when(entry)
    def _():
        for v in range(levels):
            own_load(v).start()

    barrier = pltpu.get_barrier_semaphore()
    for step in range(1, rows):
        pl.semaphore_signal(
            barrier, inc=1, device_id={"row": lax.rem(z + step, rows)}, device_id_type=MESH
        )
    pl.semaphore_signal(barrier, inc=1, device_id={"col": far}, device_id_type=MESH)
    pl.semaphore_signal(barrier, inc=1, device_id={"col": mate}, device_id_type=MESH)
    pl.semaphore_signal(barrier, inc=1, device_id={"gz": other}, device_id_type=MESH)
    first.wait()
    pl.semaphore_wait(barrier, rows + 2)

    half = width // 2
    pieces = [slice(h * half, (h + 1) * half) for h in range(2)]

    def via(r, q):
        lo = 1 - r // (rows // 2)
        rr = lo * r + (1 - lo) * (last - r)
        qq = lo * q + (1 - lo) * (last - q)
        return jnp.logical_and(qq >= 2, jnp.logical_or(rr == 1, qq == 2))

    def place(v, h):
        return remote(
            l_ref.at[v, pieces[h]], l_all.at[v, z, pieces[h]],
            l_send.at[v, h], l_recv.at[v, h, z], {"row": c},
        )

    def cross(v):
        return remote(
            l_ref.at[v, pieces[1]], crossed.at[v], x_send.at[v], x_recv.at[v], {"col": far}
        )

    def onward(v):
        return remote(
            crossed.at[v], l_all.at[v, z, pieces[1]], c_send.at[v], l_recv.at[v, 1, z], {"row": far}
        )

    via_here, via_far = via(z, c), via(z, far)
    away = jnp.logical_not(entry)
    straight = jnp.logical_and(away, jnp.logical_not(via_here))

    for v in range(levels):
        pl.when(via_here)(lambda v=v: cross(v).start())
        pl.when(away)(lambda v=v: place(v, 0).start())
        pl.when(straight)(lambda v=v: place(v, 1).start())

    own_live = pltpu.make_async_copy(live_ref, live_all.at[z], m_loc)
    own_live.start()
    live_out = []
    for step in range(1, rows):
        to = lax.rem(z + step, rows)
        live_out.append(
            remote(live_ref, live_all.at[z], m_send.at[step], m_recv.at[z], {"row": to})
        )
        live_out[-1].start()
    rm_copy = remote(rm_ref, rm_in, rm_send, rm_recv, {"gz": other})
    rm_copy.start()

    def carry_on(v):
        @pl.when(via_far)
        def _():
            cross(v).wait_recv()
            onward(v).start()

    def passes(v, a, h):
        spot = l_all.at[v, a, pieces[h]]
        post = remote(spot, spot, post_send.at[v, h, a], l_recv.at[v, h, a], {"col": far})
        relay = remote(spot, spot, relay_send.at[v, h, a], l_recv.at[v, h, a], {"col": mate})
        return post, relay

    count = rows - 1

    def place_of(k):
        mine = k // (levels * count)
        i = lax.rem(k, count)
        near = (1 - depth) * (i + 1) + depth * (i + (i + 1) // 2)
        near = low * near + (1 - low) * (last - near)
        v = mine * (k - levels * count) + (1 - mine) * (k // count)
        return v, mine * z + (1 - mine) * near

    def gather(k):
        v, a = place_of(k)
        turned = via(a, z)

        def spread(h):
            post, relay = passes(v, a, h)
            post.start()
            relay.start()

        @pl.when(entry)
        def _():
            pl.when(a == z)(lambda: own_load(v).wait())
            pl.when(a != z)(lambda: passes(v, a, 0)[1].wait_recv())
            spread(0)

            @pl.when(jnp.logical_not(turned))
            def _():
                pl.when(a != z)(lambda: passes(v, a, 1)[1].wait_recv())
                spread(1)

        @pl.when(jnp.logical_and(second, turned))
        def _():
            passes(v, a, 1)[1].wait_recv()
            spread(1)

    def take(k):
        v, a = place_of(k)
        turned = via(a, z)

        def hand(h):
            relay = passes(v, a, h)[1]
            relay.wait_recv()
            relay.start()

        pl.when(second)(lambda: hand(0))
        pl.when(jnp.logical_and(second, jnp.logical_not(turned)))(lambda: hand(1))
        pl.when(jnp.logical_and(entry, turned))(lambda: hand(1))

        @pl.when(jnp.logical_not(gate))
        def _():
            for h in range(2):
                passes(v, a, h)[1].wait_recv()

    def hop(v, a, l, side, to):
        return remote(
            part.at[v, a, l], p_in.at[v, side, a, l],
            p_send.at[v, a, l], p_recv.at[v, side, a, l], {"row": to},
        )

    inward, outward = 1 - low, low
    near_end, far_end = last * inward, last * low
    across_mid = last - z
    next_in = low + (1 - low) * (last - 1)

    def send(v, a, l):
        part[v, a, l] = own[v, a, l].astype(jnp.bfloat16)
        hop(v, a, l, inward, next_in).start()

    def item(k):
        v, a = place_of(k)
        block = l_all[v, a]
        to_layer = cm_ref[v]
        live = live_all[a, v]
        for j in range(CB):
            t = jnp.dot(
                block, u_ref[v, :, j * width : (j + 1) * width], preferred_element_type=jnp.float32
            )
            for l in range(layers):
                m = jnp.where(to_layer[:, j : j + 1] == l, live[:, j : j + 1], 0).astype(jnp.float32)
                if j == 0:
                    own[v, a, l] = t * m
                else:
                    own[v, a, l] += t * m

        @pl.when(jnp.logical_and(at_end, k < count))
        def _():
            send(v, a, other)
            pl.when(k > 0)(lambda: send(v, a, g))

        @pl.when(jnp.logical_and(at_end, k == levels * count - 1))
        def _():
            late = levels - 1
            near, mid, end = next_in, last - next_in, last - z
            for a_, l_ in ((end, other), (mid, other), (end, g), (near, other), (mid, g)):
                send(late, a_, l_)
            send(0, near, g)
            send(late, near, g)

    carry_on(0)
    gather(0)
    own_live.wait()
    for step in range(1, rows):
        src = lax.rem(z + step, rows)
        remote(live_ref, live_all.at[src], m_send.at[step], m_recv.at[src], {"row": src}).wait_recv()
    whole_u.wait()
    total = levels * rows

    def body(k, carry):
        pl.when(k == 0)(lambda: [carry_on(v) for v in range(1, levels)] and None)
        pl.when(k < total - 1)(lambda: gather(k + 1))
        take(k)
        item(k)
        return carry

    lax.fori_loop(0, total, body, 0)

    def collect(v, l, side):
        hop(v, z, l, side, z).wait_recv()
        own[v, z, l] += p_in[v, side, z, l].astype(jnp.float32)

    def forward(v, a, l, side, to):
        hop(v, a, l, side, to).wait_recv()
        part[v, a, l] = (own[v, a, l] + p_in[v, side, a, l].astype(jnp.float32)).astype(jnp.bfloat16)
        hop(v, a, l, side, to).start()

    def way(v):
        return remote(y_out.at[v], y_in.at[v], y_send.at[v], y_recv.at[v], {"gz": other})

    def trade(v):
        y_out[v] = own[v, z, other].astype(jnp.bfloat16)
        way(v).start()

    def finish(v):
        mine = own[v, z, g].astype(jnp.bfloat16).astype(jnp.float32)
        way(v).wait_recv()
        theirs = y_in[v].astype(jnp.float32)
        for f in range(FRB):
            lines = slice(f * width, (f + 1) * width)
            here = (rm_ref[v] == f).astype(jnp.float32)
            there = (rm_in[v] == f).astype(jnp.float32)
            total = here * mine + there * theirs
            out_ref[v, lines, :] = (front_ref[v, lines, :].astype(jnp.float32) - total).astype(
                out_ref.dtype
            )

    fronts.wait()
    rm_copy.wait()

    @pl.when(at_end)
    def _():
        collect(0, other, outward)
        trade(0)
        collect(0, g, outward)
        collect(1, other, outward)
        trade(1)
        finish(0)
        collect(1, g, outward)

    @pl.when(inner)
    def _():
        def ahead(v, a, l):
            forward(v, a, l, inward, across_mid)

        def back(v, l):
            forward(v, near_end, l, outward, near_end)

        collect(0, other, inward)
        ahead(0, across_mid, other)
        ahead(0, across_mid, g)
        collect(0, other, outward)
        trade(0)
        ahead(0, far_end, other)
        collect(0, g, outward)
        ahead(0, far_end, g)
        back(0, other)
        ahead(1, far_end, other)
        back(0, g)
        ahead(1, across_mid, other)
        back(1, other)
        ahead(1, far_end, g)
        collect(1, other, outward)
        collect(1, other, inward)
        trade(1)
        back(1, g)
        ahead(1, across_mid, g)
        collect(0, g, inward)
        finish(0)
        collect(1, g, outward)
        collect(1, g, inward)

    finish(1)

    for copy in live_out:
        copy.wait_send()
    for v in range(levels):
        way(v).wait_send()
        pl.when(via_here)(cross(v).wait_send)
        pl.when(via_far)(onward(v).wait_send)
        pl.when(away)(place(v, 0).wait_send)
        pl.when(straight)(place(v, 1).wait_send)

        def drain(a, carry, v=v):
            turned = via(a, z)

            @pl.when(gate)
            def _():
                for h in range(2):
                    passes(v, a, h)[1].wait_send()

            pl.when(entry)(lambda: passes(v, a, 0)[0].wait_send())
            posted = jnp.logical_or(
                jnp.logical_and(entry, jnp.logical_not(turned)), jnp.logical_and(second, turned)
            )
            pl.when(posted)(lambda: passes(v, a, 1)[0].wait_send())

            @pl.when(a != z)
            def _():
                for l in range(layers):
                    hop(v, a, l, 0, z).wait_send()

            return carry

        lax.fori_loop(0, rows, drain, 0)


def stationary(rows, cols, layers, lpanel, upanel, rowmap, colmap, blockmask, front_blocks):
    levels, _, width, depth = lpanel.shape
    bf16 = jnp.bfloat16
    vmem = pl.BlockSpec(memory_space=pltpu.VMEM)
    hbm = pl.BlockSpec(memory_space=pl.ANY)
    dma = pltpu.SemaphoreType.DMA
    return pl.pallas_call(
        functools.partial(kernel, rows, cols, layers, levels, width),
        out_shape=jax.ShapeDtypeStruct(front_blocks.shape, front_blocks.dtype),
        in_specs=[hbm, hbm, vmem, vmem, vmem, hbm],
        out_specs=vmem,
        scratch_shapes=[
            pltpu.VMEM((levels, width, depth), bf16),
            pltpu.VMEM(upanel[:, 0].shape, bf16),
            pltpu.VMEM(front_blocks.shape, bf16),
            pltpu.VMEM((levels, width // 2, depth), bf16),
            pltpu.VMEM((levels, rows, width, depth), bf16),
            pltpu.VMEM((rows,) + blockmask.shape[:1] + blockmask.shape[2:], jnp.int32),
            pltpu.VMEM((levels, rows, layers, width, width), jnp.float32),
            pltpu.VMEM((levels, rows, layers, width, width), bf16),
            pltpu.VMEM((levels, 2, rows, layers, width, width), bf16),
            pltpu.VMEM((levels, width, width), bf16),
            pltpu.VMEM((levels, width, width), bf16),
            pltpu.VMEM(rowmap.shape, jnp.int32),
            dma((3,)),
            dma((levels,)),
            dma((levels,)),
            dma((levels,)),
            dma((levels,)),
            dma((levels, 2)),
            dma((levels, 2, rows)),
            dma((levels, 2, rows)),
            dma((levels, 2, rows)),
            dma((rows,)),
            dma((rows,)),
            dma,
            dma((levels, rows, layers)),
            dma((levels, 2, rows, layers)),
            dma((levels,)),
            dma((levels,)),
            dma,
            dma,
        ],
        compiler_params=pltpu.CompilerParams(collective_id=0, has_side_effects=True),
    )(lpanel[:, 0], upanel[:, 0], colmap, blockmask[:, 0], rowmap, front_blocks)


def solution(mesh):
    rows, cols, layers = mesh.shape["row"], mesh.shape["col"], mesh.shape["gz"]
    body = general
    if rows == cols == 2 * layers and layers == 2:
        body = functools.partial(stationary, rows, cols, layers)
    return jax.shard_map(
        body,
        mesh=mesh,
        in_specs=(
            P(None, "gz", "row", "col"),
            P(None, "gz", "row", "col"),
            P(None, "gz", "row"),
            P(None, "gz", "col"),
            P(None, "gz", "row", "col"),
            P(None, "row", ("gz", "col")),
        ),
        out_specs=P(None, "row", ("gz", "col")),
        check_vma=False,
    )
```

time: 67.6 us -> 73.1 us (1.081)
  Pallas kernels: 64.3 us -> 69.8 us
    pallas_call x1, Pallas kernels: 64.3 us -> 69.8 us  [stationary(): pl.pallas_call(functools.partial(kernel, rows, cols, layers, levels, widt...]
    unnamed x1 -> x2, local copies, waits for them, and re-layouts: 1.87 us -> 3.16 us
    squeeze x1 -> x0, local copies, waits for them, and re-layouts: 1.3 us -> none  [stationary(): rowmap[:, 0]]
where the time goes in v1:
time: 73.1 us; the launch traced here: 73 us
  Pallas kernels  69.8 us (95%)
  local copies, waits for them, and re-layouts  3.16 us (4%)
    pallas_call x1, Pallas kernels, stationary(): pl.pallas_call(functools.partial(kernel, rows, cols, layers, levels, widt...  69.8 us
    unnamed x2, local copies, waits for them, and re-layouts  3.16 us

profile of v1, /device:TPU:0, one launch (start us, length us, event | category | flops | bytes accessed | tf_op | source)
XLA Modules:
  0.0 73.0 jit_solution(5302327068902497627)
XLA Ops:
  0.0 1.3 %copy.8.rm_ref = s32[2,1,1]{2,1,0:T(1,128)} copy(s32[2,1,1]{0,2,1:T(1,128)} %param.8) | data formatting | bytes 16 | tf_op args[2]
  1.3 69.8 %shard_map.64 = bf16[2,512,256]{2,1,0:T(8,128)(2,1)} custom-call(bf16[2,256,512]{2,1,0:T(8,128)(2,1)} %bitcast.6, bf16[2,512,1024]{2,1,0:T(8,128)(2,1)} %bitcast.5, s32[2,1,4]{2,1,0:T(1,128)} %cm_ref.1, s32[2,1,4]{2,1,0:T(1,128)} %bitcast.7, s32[2,1,1]{2,1,0:T(1,128)} %copy.8.rm_ref, bf16[2,512,256]{2,1,0:T(8,128)(2,1)} %front_hbm.1), custom_call_target="tpu_custom_call" | custom-call | tf_op jit(solution)/shard_map/pallas_call | solution.py:397
  71.1 1.9 %copy.10 = bf16[2,512,256]{2,1,0:T(8,128)(2,1)} copy(bf16[2,512,256]{2,1,0:T(8,128)(2,1)} %shard_map.64) | data formatting | bytes 1048576

commit v2 on v1

--- a/solution.py
+++ b/solution.py
@@ -134,10 +134,13 @@
     away = jnp.logical_not(entry)
     straight = jnp.logical_and(away, jnp.logical_not(via_here))
 
-    for v in range(levels):
-        pl.when(via_here)(lambda v=v: cross(v).start())
-        pl.when(away)(lambda v=v: place(v, 0).start())
-        pl.when(straight)(lambda v=v: place(v, 1).start())
+    def launch(v):
+        pl.when(via_here)(lambda: cross(v).start())
+        pl.when(away)(lambda: place(v, 0).start())
+        pl.when(straight)(lambda: place(v, 1).start())
+
+    launch(0)
+    pl.when(at_end)(lambda: launch(1))
 
     own_live = pltpu.make_async_copy(live_ref, live_all.at[z], m_loc)
     own_live.start()
@@ -247,37 +250,17 @@
                 else:
                     own[v, a, l] += t * m
 
-        @pl.when(jnp.logical_and(at_end, k < count))
-        def _():
-            send(v, a, other)
-            pl.when(k > 0)(lambda: send(v, a, g))
-
-        @pl.when(jnp.logical_and(at_end, k == levels * count - 1))
-        def _():
-            late = levels - 1
-            near, mid, end = next_in, last - next_in, last - z
-            for a_, l_ in ((end, other), (mid, other), (end, g), (near, other), (mid, g)):
-                send(late, a_, l_)
-            send(0, near, g)
-            send(late, near, g)
 
     carry_on(0)
+    pl.when(at_end)(lambda: carry_on(1))
     gather(0)
     own_live.wait()
     for step in range(1, rows):
         src = lax.rem(z + step, rows)
         remote(live_ref, live_all.at[src], m_send.at[step], m_recv.at[src], {"row": src}).wait_recv()
     whole_u.wait()
-    total = levels * rows
-
-    def body(k, carry):
-        pl.when(k == 0)(lambda: [carry_on(v) for v in range(1, levels)] and None)
-        pl.when(k < total - 1)(lambda: gather(k + 1))
-        take(k)
-        item(k)
-        return carry
-
-    lax.fori_loop(0, total, body, 0)
+    rm_copy.wait()
+    fronts.wait()
 
     def collect(v, l, side):
         hop(v, z, l, side, z).wait_recv()
@@ -308,8 +291,81 @@
                 out_ref.dtype
             )
 
-    fronts.wait()
-    rm_copy.wait()
+
+    def ahead(v, a, l):
+        forward(v, a, l, inward, across_mid)
+
+    def back(v, l):
+        forward(v, near_end, l, outward, near_end)
+
+    near, mid, end = next_in, last - next_in, last - z
+    early = {0: ((near, other),), 1: ((mid, other), (mid, g)), 2: ((end, other), (end, g))}
+
+    def edge_step(k):
+        for a, l in early.get(k, ()):
+            send(0, a, l)
+        if k == 2 * count - 1:
+            for a, l in ((end, other), (mid, other), (end, g), (near, other), (mid, g)):
+                send(1, a, l)
+            send(0, near, g)
+            send(1, near, g)
+
+    def shared_step(k):
+        if k == 0:
+            pl.when(inner)(lambda: launch(1))
+            gather(1)
+            gather(2)
+        if k == 1:
+            pl.when(inner)(lambda: carry_on(1))
+        if k == 2:
+            gather(3)
+        if k == 3:
+            for n in range(4, levels * rows):
+                gather(n)
+
+    def inner_step(k):
+        if k == 3:
+            ahead(0, across_mid, other)
+            ahead(0, across_mid, g)
+        if k == 4:
+            ahead(0, far_end, other)
+        if k == 5:
+            ahead(0, far_end, g)
+            back(0, other)
+            ahead(1, far_end, other)
+            back(0, g)
+        if k == 6:
+            collect(0, other, inward)
+            collect(0, other, outward)
+            trade(0)
+            ahead(1, across_mid, other)
+            back(1, other)
+            collect(0, g, outward)
+            ahead(1, far_end, g)
+        if k == 7:
+            collect(1, other, outward)
+            collect(1, other, inward)
+            trade(1)
+            back(1, g)
+            ahead(1, across_mid, g)
+            collect(0, g, inward)
+            finish(0)
+            collect(1, g, outward)
+            collect(1, g, inward)
+
+    def body(k, carry):
+        take(k)
+        item(k)
+        for step in range(levels * rows):
+            @pl.when(k == step)
+            def _(step=step):
+                pl.when(at_end)(lambda: edge_step(step))
+                shared_step(step)
+                pl.when(inner)(lambda: inner_step(step))
+
+        return carry
+
+    lax.fori_loop(0, levels * rows, body, 0)
 
     @pl.when(at_end)
     def _():
@@ -320,38 +376,6 @@
         trade(1)
         finish(0)
         collect(1, g, outward)
-
-    @pl.when(inner)
-    def _():
-        def ahead(v, a, l):
-            forward(v, a, l, inward, across_mid)
-
-        def back(v, l):
-            forward(v, near_end, l, outward, near_end)
-
-        collect(0, other, inward)
-        ahead(0, across_mid, other)
-        ahead(0, across_mid, g)
-        collect(0, other, outward)
-        trade(0)
-        ahead(0, far_end, other)
-        collect(0, g, outward)
-        ahead(0, far_end, g)
-        back(0, other)
-        ahead(1, far_end, other)
-        back(0, g)
-        ahead(1, across_mid, other)
-        back(1, other)
-        ahead(1, far_end, g)
-        collect(1, other, outward)
-        collect(1, other, inward)
-        trade(1)
-        back(1, g)
-        ahead(1, across_mid, g)
-        collect(0, g, inward)
-        finish(0)
-        collect(1, g, outward)
-        collect(1, g, inward)
 
     finish(1)
 

time: 73.1 us -> 64.3 us (0.88)
  Pallas kernels: 69.8 us -> 61 us
    pallas_call x1, Pallas kernels: 69.8 us -> 61 us  [stationary(): pl.pallas_call(functools.partial(kernel, rows, cols, layers, levels, widt...]
where the time goes in v2:
time: 64.3 us; the launch traced here: 64.1 us
  Pallas kernels  61 us (95%)
  local copies, waits for them, and re-layouts  3.16 us (5%)
    pallas_call x1, Pallas kernels, stationary(): pl.pallas_call(functools.partial(kernel, rows, cols, layers, levels, widt...  61 us
    unnamed x2, local copies, waits for them, and re-layouts  3.16 us

profile of v2, /device:TPU:0, one launch (start us, length us, event | category | flops | bytes accessed | tf_op | source)
XLA Modules:
  0.0 64.1 jit_solution(5007878088482824999)
XLA Ops:
  0.0 1.3 %copy.8.rm_ref = s32[2,1,1]{2,1,0:T(1,128)} copy(s32[2,1,1]{0,2,1:T(1,128)} %param.8) | data formatting | bytes 16 | tf_op args[2]
  1.3 61.0 %shard_map.64 = bf16[2,512,256]{2,1,0:T(8,128)(2,1)} custom-call(bf16[2,256,512]{2,1,0:T(8,128)(2,1)} %bitcast.6, bf16[2,512,1024]{2,1,0:T(8,128)(2,1)} %bitcast.5, s32[2,1,4]{2,1,0:T(1,128)} %cm_ref.1, s32[2,1,4]{2,1,0:T(1,128)} %bitcast.7, s32[2,1,1]{2,1,0:T(1,128)} %copy.8.rm_ref, bf16[2,512,256]{2,1,0:T(8,128)(2,1)} %front_hbm.1), custom_call_target="tpu_custom_call" | custom-call | tf_op jit(solution)/shard_map/pallas_call | solution.py:421
  62.3 1.9 %copy.10 = bf16[2,512,256]{2,1,0:T(8,128)(2,1)} copy(bf16[2,512,256]{2,1,0:T(8,128)(2,1)} %shard_map.64) | data formatting | bytes 1048576

commit v3 on v2

--- a/solution.py
+++ b/solution.py
@@ -54,10 +54,11 @@
 
 def kernel(
     rows, cols, layers, levels, width,
-    l_hbm, u_hbm, cm_ref, live_ref, rm_ref, front_hbm, out_ref,
+    l_hbm, u_hbm, cm_hbm, live_hbm, rm_hbm, front_hbm, out_ref,
+    cm_ref, live_ref, rm_ref,
     l_ref, u_ref, front_ref, crossed, l_all, live_all, own, part, p_in, y_out, y_in, rm_in,
     in_sem, own_sem, x_send, x_recv, c_send, l_send, l_recv, post_send, relay_send,
-    m_send, m_recv, m_loc, p_send, p_recv, y_send, y_recv, rm_send, rm_recv,
+    m_send, m_recv, p_send, p_recv, y_send, y_recv, rm_send, rm_recv,
 ):
     z = lax.axis_index("row")
     c = lax.axis_index("col")
@@ -79,8 +80,25 @@
             device_id=where, device_id_type=MESH,
         )
 
+    barrier = pltpu.get_barrier_semaphore()
+    for step in range(1, rows):
+        pl.semaphore_signal(
+            barrier, inc=1, device_id={"row": lax.rem(z + step, rows)}, device_id_type=MESH
+        )
+    pl.semaphore_signal(barrier, inc=1, device_id={"col": far}, device_id_type=MESH)
+    pl.semaphore_signal(barrier, inc=1, device_id={"col": mate}, device_id_type=MESH)
+    pl.semaphore_signal(barrier, inc=1, device_id={"gz": other}, device_id_type=MESH)
+
     first = pltpu.make_async_copy(l_hbm, l_ref, in_sem.at[0])
     first.start()
+    small = [
+        pltpu.make_async_copy(src, dst, in_sem.at[3 + i])
+        for i, (src, dst) in enumerate(
+            ((live_hbm, live_ref), (rm_hbm, rm_ref), (cm_hbm, cm_ref), (live_hbm, live_all.at[z]))
+        )
+    ]
+    for copy in small:
+        copy.start()
     whole_u = pltpu.make_async_copy(u_hbm, u_ref, in_sem.at[1])
     whole_u.start()
     fronts = pltpu.make_async_copy(front_hbm, front_ref, in_sem.at[2])
@@ -94,25 +112,16 @@
         for v in range(levels):
             own_load(v).start()
 
-    barrier = pltpu.get_barrier_semaphore()
-    for step in range(1, rows):
-        pl.semaphore_signal(
-            barrier, inc=1, device_id={"row": lax.rem(z + step, rows)}, device_id_type=MESH
-        )
-    pl.semaphore_signal(barrier, inc=1, device_id={"col": far}, device_id_type=MESH)
-    pl.semaphore_signal(barrier, inc=1, device_id={"col": mate}, device_id_type=MESH)
-    pl.semaphore_signal(barrier, inc=1, device_id={"gz": other}, device_id_type=MESH)
+    for copy in small:
+        copy.wait()
     first.wait()
     pl.semaphore_wait(barrier, rows + 2)
 
     half = width // 2
     pieces = [slice(h * half, (h + 1) * half) for h in range(2)]
 
-    def via(r, q):
-        lo = 1 - r // (rows // 2)
-        rr = lo * r + (1 - lo) * (last - r)
-        qq = lo * q + (1 - lo) * (last - q)
-        return jnp.logical_and(qq >= 2, jnp.logical_or(rr == 1, qq == 2))
+    def short(r, q):
+        return jnp.logical_and(r * (last - r) > 0, q * (last - q) == 0)
 
     def place(v, h):
         return remote(
@@ -130,20 +139,23 @@
             crossed.at[v], l_all.at[v, z, pieces[1]], c_send.at[v], l_recv.at[v, 1, z], {"row": far}
         )
 
-    via_here, via_far = via(z, c), via(z, far)
-    away = jnp.logical_not(entry)
-    straight = jnp.logical_and(away, jnp.logical_not(via_here))
+    away, helper = jnp.logical_not(entry), jnp.logical_not(second)
+    direct, helps_direct = short(z, c), short(z, far)
+    crosses = [jnp.logical_and(away, jnp.logical_not(direct)), away]
+    helps = [jnp.logical_and(helper, jnp.logical_not(helps_direct)), helper]
 
     def launch(v):
-        pl.when(via_here)(lambda: cross(v).start())
-        pl.when(away)(lambda: place(v, 0).start())
-        pl.when(straight)(lambda: place(v, 1).start())
-
-    launch(0)
-    pl.when(at_end)(lambda: launch(1))
-
-    own_live = pltpu.make_async_copy(live_ref, live_all.at[z], m_loc)
-    own_live.start()
+        place(v, 0).start()
+        pl.when(crosses[v])(lambda: cross(v).start())
+        if v == 0:
+            pl.when(direct)(lambda: place(v, 1).start())
+
+    def carry_on(v):
+        @pl.when(helps[v])
+        def _():
+            cross(v).wait_recv()
+            onward(v).start()
+
     live_out = []
     for step in range(1, rows):
         to = lax.rem(z + step, rows)
@@ -153,12 +165,16 @@
         live_out[-1].start()
     rm_copy = remote(rm_ref, rm_in, rm_send, rm_recv, {"gz": other})
     rm_copy.start()
-
-    def carry_on(v):
-        @pl.when(via_far)
-        def _():
-            cross(v).wait_recv()
-            onward(v).start()
+    gap = (z - c) * (z - c)
+    beside = gap == 1
+    patient = jnp.logical_and(gap >= 4, c * (last - c) == 0)
+    eager = jnp.logical_and(away, jnp.logical_not(patient))
+    lead = jnp.logical_and(beside, jnp.logical_or(at_end, direct))
+    outer_two = jnp.logical_and(at_end, gap == 4)
+    outer_three = gap == 9
+    later = jnp.logical_and(inner, jnp.logical_and(away, jnp.logical_not(lead)))
+    pl.when(eager)(lambda: launch(0))
+    pl.when(lead)(lambda: launch(1))
 
     def passes(v, a, h):
         spot = l_all.at[v, a, pieces[h]]
@@ -170,49 +186,65 @@
 
     def place_of(k):
         mine = k // (levels * count)
-        i = lax.rem(k, count)
+        first = 1 - (k + levels) // (2 * levels)
+        rest = k - levels
+        v = first * k + (1 - first) * (rest // levels)
+        step = lax.rem(rest + 2 * levels, levels)
+        i = (1 - first) * (1 + step + v * (1 - 2 * step))
         near = (1 - depth) * (i + 1) + depth * (i + (i + 1) // 2)
         near = low * near + (1 - low) * (last - near)
-        v = mine * (k - levels * count) + (1 - mine) * (k // count)
+        v = mine * (k - levels * count) + (1 - mine) * v
         return v, mine * z + (1 - mine) * near
 
-    def gather(k):
+    def turned(v, a, h):
+        if h == 0:
+            return a < 0
+        plain = jnp.logical_or(a == z, jnp.logical_and(v == 0, short(a, z)))
+        return jnp.logical_not(plain)
+
+    def spread(v, a, h):
+        post, relay = passes(v, a, h)
+        post.start()
+        relay.start()
+
+    def gather_entry(k):
         v, a = place_of(k)
-        turned = via(a, z)
-
-        def spread(h):
-            post, relay = passes(v, a, h)
-            post.start()
-            relay.start()
 
         @pl.when(entry)
         def _():
             pl.when(a == z)(lambda: own_load(v).wait())
-            pl.when(a != z)(lambda: passes(v, a, 0)[1].wait_recv())
-            spread(0)
-
-            @pl.when(jnp.logical_not(turned))
-            def _():
-                pl.when(a != z)(lambda: passes(v, a, 1)[1].wait_recv())
-                spread(1)
-
-        @pl.when(jnp.logical_and(second, turned))
-        def _():
-            passes(v, a, 1)[1].wait_recv()
-            spread(1)
+            for h in range(2):
+                @pl.when(jnp.logical_not(turned(v, a, h)))
+                def _(h=h):
+                    pl.when(a != z)(lambda: passes(v, a, h)[1].wait_recv())
+                    spread(v, a, h)
+
+    def gather_second(k):
+        v, a = place_of(k)
+        for h in range(2):
+            @pl.when(jnp.logical_and(second, turned(v, a, h)))
+            def _(h=h):
+                passes(v, a, h)[1].wait_recv()
+                spread(v, a, h)
+
+    def gather(k):
+        gather_entry(k)
+        gather_second(k)
 
     def take(k):
         v, a = place_of(k)
-        turned = via(a, z)
 
         def hand(h):
             relay = passes(v, a, h)[1]
             relay.wait_recv()
             relay.start()
 
-        pl.when(second)(lambda: hand(0))
-        pl.when(jnp.logical_and(second, jnp.logical_not(turned)))(lambda: hand(1))
-        pl.when(jnp.logical_and(entry, turned))(lambda: hand(1))
+        for h in range(2):
+            there = turned(v, a, h)
+            taken = jnp.logical_or(
+                jnp.logical_and(second, jnp.logical_not(there)), jnp.logical_and(entry, there)
+            )
+            pl.when(taken)(lambda h=h: hand(h))
 
         @pl.when(jnp.logical_not(gate))
         def _():
@@ -251,13 +283,32 @@
                     own[v, a, l] += t * m
 
 
-    carry_on(0)
-    pl.when(at_end)(lambda: carry_on(1))
-    gather(0)
-    own_live.wait()
-    for step in range(1, rows):
-        src = lax.rem(z + step, rows)
-        remote(live_ref, live_all.at[src], m_send.at[step], m_recv.at[src], {"row": src}).wait_recv()
+    def hear(src):
+        remote(live_ref, live_all.at[src], m_send.at[1], m_recv.at[src], {"row": src}).wait_recv()
+
+    spare = jnp.logical_not(gate)
+    busy_inner = jnp.logical_and(inner, gate)
+    busy_end = jnp.logical_and(at_end, gate)
+    pl.when(inner)(lambda: carry_on(0))
+    hear(place_of(0)[1])
+    pl.when(patient)(lambda: launch(0))
+    pl.when(outer_two)(lambda: launch(1))
+    gather_entry(0)
+
+    @pl.when(inner)
+    def _():
+        gather_second(0)
+        gather(2)
+        gather(1)
+
+    @pl.when(at_end)
+    def _():
+        carry_on(0)
+        gather_second(1)
+
+    pl.when(later)(lambda: launch(1))
+    pl.when(outer_three)(lambda: launch(1))
+    pl.when(spare)(lambda: carry_on(1))
     whole_u.wait()
     rm_copy.wait()
     fronts.wait()
@@ -284,8 +335,8 @@
         theirs = y_in[v].astype(jnp.float32)
         for f in range(FRB):
             lines = slice(f * width, (f + 1) * width)
-            here = (rm_ref[v] == f).astype(jnp.float32)
-            there = (rm_in[v] == f).astype(jnp.float32)
+            here = (rm_ref[0, :, v : v + 1] == f).astype(jnp.float32)
+            there = (rm_in[0, :, v : v + 1] == f).astype(jnp.float32)
             total = here * mine + there * theirs
             out_ref[v, lines, :] = (front_ref[v, lines, :].astype(jnp.float32) - total).astype(
                 out_ref.dtype
@@ -299,55 +350,77 @@
         forward(v, near_end, l, outward, near_end)
 
     near, mid, end = next_in, last - next_in, last - z
-    early = {0: ((near, other),), 1: ((mid, other), (mid, g)), 2: ((end, other), (end, g))}
+    early = {
+        0: ((0, near, other),),
+        1: ((1, near, other),),
+        2: ((0, mid, other),),
+        3: ((0, end, other), (0, end, g)),
+        4: ((1, end, other), (1, end, g)),
+        5: ((1, mid, other), (0, mid, g), (1, mid, g), (0, near, g), (1, near, g)),
+    }
 
     def edge_step(k):
-        for a, l in early.get(k, ()):
-            send(0, a, l)
-        if k == 2 * count - 1:
-            for a, l in ((end, other), (mid, other), (end, g), (near, other), (mid, g)):
-                send(1, a, l)
-            send(0, near, g)
-            send(1, near, g)
+        for v, a, l in early.get(k, ()):
+            send(v, a, l)
+
+    def edge_gather(k):
+        if k == 0:
+            pl.when(busy_end)(lambda: carry_on(1))
+            gather_second(2)
+            gather_entry(1)
+            gather_entry(2)
+        if k == 1:
+            gather(3)
+        if k == 2:
+            gather_entry(4)
+        if k == 3:
+            gather_second(4)
+            gather(5)
+            gather_entry(6)
+            gather_entry(7)
+
+    def inner_gather(k):
+        if k == 0:
+            pl.when(busy_inner)(lambda: carry_on(1))
+            gather(3)
+        if k == 1:
+            gather(4)
+        if k == 2:
+            gather(5)
+        if k == 3:
+            gather_entry(6)
+            gather_entry(7)
 
     def shared_step(k):
-        if k == 0:
-            pl.when(inner)(lambda: launch(1))
-            gather(1)
-            gather(2)
-        if k == 1:
-            pl.when(inner)(lambda: carry_on(1))
-        if k == 2:
-            gather(3)
-        if k == 3:
-            for n in range(4, levels * rows):
-                gather(n)
+        pl.when(at_end)(lambda: edge_gather(k))
+        pl.when(inner)(lambda: inner_gather(k))
+        if k in (1, 2):
+            hear(place_of(k + 1)[1])
 
     def inner_step(k):
         if k == 3:
             ahead(0, across_mid, other)
-            ahead(0, across_mid, g)
-        if k == 4:
             ahead(0, far_end, other)
         if k == 5:
             ahead(0, far_end, g)
+            ahead(1, far_end, other)
             back(0, other)
-            ahead(1, far_end, other)
-            back(0, g)
         if k == 6:
             collect(0, other, inward)
             collect(0, other, outward)
             trade(0)
+            ahead(1, far_end, g)
+            back(0, g)
+        if k == 7:
             ahead(1, across_mid, other)
             back(1, other)
+            ahead(0, across_mid, g)
+            back(1, g)
+            collect(1, other, inward)
+            collect(1, other, outward)
+            trade(1)
+            ahead(1, across_mid, g)
             collect(0, g, outward)
-            ahead(1, far_end, g)
-        if k == 7:
-            collect(1, other, outward)
-            collect(1, other, inward)
-            trade(1)
-            back(1, g)
-            ahead(1, across_mid, g)
             collect(0, g, inward)
             finish(0)
             collect(1, g, outward)
@@ -383,24 +456,21 @@
         copy.wait_send()
     for v in range(levels):
         way(v).wait_send()
-        pl.when(via_here)(cross(v).wait_send)
-        pl.when(via_far)(onward(v).wait_send)
+        pl.when(crosses[v])(cross(v).wait_send)
+        pl.when(helps[v])(onward(v).wait_send)
         pl.when(away)(place(v, 0).wait_send)
-        pl.when(straight)(place(v, 1).wait_send)
+        if v == 0:
+            pl.when(direct)(place(v, 1).wait_send)
 
         def drain(a, carry, v=v):
-            turned = via(a, z)
-
-            @pl.when(gate)
-            def _():
-                for h in range(2):
-                    passes(v, a, h)[1].wait_send()
-
-            pl.when(entry)(lambda: passes(v, a, 0)[0].wait_send())
-            posted = jnp.logical_or(
-                jnp.logical_and(entry, jnp.logical_not(turned)), jnp.logical_and(second, turned)
-            )
-            pl.when(posted)(lambda: passes(v, a, 1)[0].wait_send())
+            for h in range(2):
+                post, relay = passes(v, a, h)
+                pl.when(gate)(relay.wait_send)
+                there = turned(v, a, h)
+                posted = jnp.logical_or(
+                    jnp.logical_and(entry, jnp.logical_not(there)), jnp.logical_and(second, there)
+                )
+                pl.when(posted)(post.wait_send)
 
             @pl.when(a != z)
             def _():
@@ -421,9 +491,12 @@
     return pl.pallas_call(
         functools.partial(kernel, rows, cols, layers, levels, width),
         out_shape=jax.ShapeDtypeStruct(front_blocks.shape, front_blocks.dtype),
-        in_specs=[hbm, hbm, vmem, vmem, vmem, hbm],
+        in_specs=[hbm] * 6,
         out_specs=vmem,
         scratch_shapes=[
+            pltpu.VMEM(colmap.shape, jnp.int32),
+            pltpu.VMEM((levels,) + blockmask.shape[2:], jnp.int32),
+            pltpu.VMEM((1, 1, levels), jnp.int32),
             pltpu.VMEM((levels, width, depth), bf16),
             pltpu.VMEM(upanel[:, 0].shape, bf16),
             pltpu.VMEM(front_blocks.shape, bf16),
@@ -435,8 +508,8 @@
             pltpu.VMEM((levels, 2, rows, layers, width, width), bf16),
             pltpu.VMEM((levels, width, width), bf16),
             pltpu.VMEM((levels, width, width), bf16),
-            pltpu.VMEM(rowmap.shape, jnp.int32),
-            dma((3,)),
+            pltpu.VMEM((1, 1, levels), jnp.int32),
+            dma((7,)),
             dma((levels,)),
             dma((levels,)),
             dma((levels,)),
@@ -447,7 +520,6 @@
             dma((levels, 2, rows)),
             dma((rows,)),
             dma((rows,)),
-            dma,
             dma((levels, rows, layers)),
             dma((levels, 2, rows, layers)),
             dma((levels,)),
@@ -456,7 +528,10 @@
             dma,
         ],
         compiler_params=pltpu.CompilerParams(collective_id=0, has_side_effects=True),
-    )(lpanel[:, 0], upanel[:, 0], colmap, blockmask[:, 0], rowmap, front_blocks)
+    )(
+        lpanel[:, 0], upanel[:, 0], colmap, blockmask[:, 0], jnp.transpose(rowmap, (1, 2, 0)),
+        front_blocks,
+    )
 
 
 def solution(mesh):

time: 64.3 us -> 56 us (0.87)
  Pallas kernels: 61 us -> 54 us
  local copies, waits for them, and re-layouts: 3.16 us -> 1.87 us
    pallas_call x1, Pallas kernels: 61 us -> 54 us  [stationary(): pl.pallas_call(functools.partial(kernel, rows, cols, layers, levels, widt...]
    unnamed x2 -> x1, local copies, waits for them, and re-layouts: 3.16 us -> 1.87 us
where the time goes in v3:
time: 56 us; the launch traced here: 55.8 us
  Pallas kernels  54 us (96%)
  local copies, waits for them, and re-layouts  1.87 us (3%)
    pallas_call x1, Pallas kernels, stationary(): pl.pallas_call(functools.partial(kernel, rows, cols, layers, levels, widt...  54 us
    unnamed x1, local copies, waits for them, and re-layouts  1.87 us

profile of v3, /device:TPU:0, one launch (start us, length us, event | category | flops | bytes accessed | tf_op | source)
XLA Modules:
  0.0 55.8 jit_solution(14837964265106504516)
XLA Ops:
  0.0 54.0 %shard_map.64 = bf16[2,512,256]{2,1,0:T(8,128)(2,1)} custom-call(bf16[2,256,512]{2,1,0:T(8,128)(2,1)} %bitcast.7, bf16[2,512,1024]{2,1,0:T(8,128)(2,1)} %bitcast.6, s32[2,1,4]{2,1,0:T(1,128)} %cm_hbm.1, s32[2,1,4]{2,1,0:T(1,128)} %bitcast.8, s32[1,1,2]{2,1,0:T(1,128)} %bitcast.9, bf16[2,512,256]{2,1,0:T(8,128)(2,1)} %front_hbm.1), custom_call_target="tpu_custom_call" | custom-call | tf_op jit(solution)/shard_map/pallas_call | solution.py:491
  54.0 1.9 %copy.9 = bf16[2,512,256]{2,1,0:T(8,128)(2,1)} copy(bf16[2,512,256]{2,1,0:T(8,128)(2,1)} %shard_map.64) | data formatting | bytes 1048576

commit v4 on v3

--- a/solution.py
+++ b/solution.py
@@ -59,6 +59,7 @@
     l_ref, u_ref, front_ref, crossed, l_all, live_all, own, part, p_in, y_out, y_in, rm_in,
     in_sem, own_sem, x_send, x_recv, c_send, l_send, l_recv, post_send, relay_send,
     m_send, m_recv, p_send, p_recv, y_send, y_recv, rm_send, rm_recv,
+    turn, stash, f_send, f_recv, g_send,
 ):
     z = lax.axis_index("row")
     c = lax.axis_index("col")
@@ -120,41 +121,45 @@
     half = width // 2
     pieces = [slice(h * half, (h + 1) * half) for h in range(2)]
 
-    def short(r, q):
-        return jnp.logical_and(r * (last - r) > 0, q * (last - q) == 0)
-
     def place(v, h):
         return remote(
             l_ref.at[v, pieces[h]], l_all.at[v, z, pieces[h]],
             l_send.at[v, h], l_recv.at[v, h, z], {"row": c},
         )
 
-    def cross(v):
+    def cross(v, h):
         return remote(
-            l_ref.at[v, pieces[1]], crossed.at[v], x_send.at[v], x_recv.at[v], {"col": far}
-        )
-
-    def onward(v):
+            l_ref.at[v, pieces[h]], crossed.at[v, pieces[h]],
+            x_send.at[v, h], x_recv.at[v, h], {"col": far},
+        )
+
+    def onward(v, h):
         return remote(
-            crossed.at[v], l_all.at[v, z, pieces[1]], c_send.at[v], l_recv.at[v, 1, z], {"row": far}
-        )
-
-    away, helper = jnp.logical_not(entry), jnp.logical_not(second)
-    direct, helps_direct = short(z, c), short(z, far)
-    crosses = [jnp.logical_and(away, jnp.logical_not(direct)), away]
-    helps = [jnp.logical_and(helper, jnp.logical_not(helps_direct)), helper]
+            crossed.at[v, pieces[h]], l_all.at[v, z, pieces[h]],
+            c_send.at[v, h], l_recv.at[v, h, z], {"row": far},
+        )
+
+    def routes(q):
+        central = q * (last - q) > 0
+        both = jnp.logical_and(jnp.logical_and(inner, central), q != z)
+        one = jnp.logical_and(jnp.logical_and(at_end, central), (q - z) * (q - z) == 4)
+        return both, jnp.logical_or(both, one)
+
+    away = jnp.logical_not(entry)
+    crosses, helps = routes(c), routes(far)
+    places = [jnp.logical_and(away, jnp.logical_not(flag)) for flag in crosses]
 
     def launch(v):
-        place(v, 0).start()
-        pl.when(crosses[v])(lambda: cross(v).start())
-        if v == 0:
-            pl.when(direct)(lambda: place(v, 1).start())
+        for h in range(2):
+            pl.when(places[h])(lambda h=h: place(v, h).start())
+            pl.when(crosses[h])(lambda h=h: cross(v, h).start())
 
     def carry_on(v):
-        @pl.when(helps[v])
-        def _():
-            cross(v).wait_recv()
-            onward(v).start()
+        for h in range(2):
+            @pl.when(helps[h])
+            def _(h=h):
+                cross(v, h).wait_recv()
+                onward(v, h).start()
 
     live_out = []
     for step in range(1, rows):
@@ -166,15 +171,48 @@
     rm_copy = remote(rm_ref, rm_in, rm_send, rm_recv, {"gz": other})
     rm_copy.start()
     gap = (z - c) * (z - c)
-    beside = gap == 1
-    patient = jnp.logical_and(gap >= 4, c * (last - c) == 0)
-    eager = jnp.logical_and(away, jnp.logical_not(patient))
-    lead = jnp.logical_and(beside, jnp.logical_or(at_end, direct))
-    outer_two = jnp.logical_and(at_end, gap == 4)
-    outer_three = gap == 9
-    later = jnp.logical_and(inner, jnp.logical_and(away, jnp.logical_not(lead)))
-    pl.when(eager)(lambda: launch(0))
-    pl.when(lead)(lambda: launch(1))
+    to_end = c * (last - c) == 0
+    distant = gap == 9
+    late = jnp.logical_and(inner, jnp.logical_and(gap == 4, to_end))
+    opener = jnp.logical_and(inner, jnp.logical_and(gap == 1, to_end))
+    nearby = jnp.logical_and(away, jnp.logical_not(distant))
+    lead = jnp.logical_and(nearby, jnp.logical_not(late))
+    near_end, far_end = last * (1 - low), last * low
+    next_in = low + (1 - low) * (last - 1)
+
+    def deposit(v):
+        return remote(l_ref.at[v], stash.at[v], f_send.at[v], f_recv.at[v], {"row": next_in})
+
+    def pick_up(v, h):
+        return remote(
+            stash.at[v, pieces[h]], l_all.at[v, near_end, pieces[h]],
+            g_send.at[v, h], l_recv.at[v, h, near_end], {"row": c},
+        )
+
+    @pl.when(distant)
+    def _():
+        for v in range(levels):
+            deposit(v).start()
+
+    @pl.when(lead)
+    def _():
+        for v in range(levels):
+            launch(v)
+
+    @pl.when(opener)
+    def _():
+        place(1, 0).wait_send()
+        pl.semaphore_signal(turn, inc=1, device_id={"row": last - z}, device_id_type=MESH)
+
+    @pl.when(late)
+    def _():
+        pl.semaphore_wait(turn, 1)
+        launch(0)
+        for v in range(levels):
+            deposit(v).wait_recv()
+            for h in range(2):
+                pick_up(v, h).start()
+        launch(1)
 
     def passes(v, a, h):
         spot = l_all.at[v, a, pieces[h]]
@@ -197,10 +235,8 @@
         return v, mine * z + (1 - mine) * near
 
     def turned(v, a, h):
-        if h == 0:
-            return a < 0
-        plain = jnp.logical_or(a == z, jnp.logical_and(v == 0, short(a, z)))
-        return jnp.logical_not(plain)
+        both = a == last - z
+        return jnp.logical_and(inner, both if h == 0 else jnp.logical_or(both, (a - z) * (a - z) == 4))
 
     def spread(v, a, h):
         post, relay = passes(v, a, h)
@@ -258,9 +294,7 @@
         )
 
     inward, outward = 1 - low, low
-    near_end, far_end = last * inward, last * low
     across_mid = last - z
-    next_in = low + (1 - low) * (last - 1)
 
     def send(v, a, l):
         part[v, a, l] = own[v, a, l].astype(jnp.bfloat16)
@@ -286,29 +320,16 @@
     def hear(src):
         remote(live_ref, live_all.at[src], m_send.at[1], m_recv.at[src], {"row": src}).wait_recv()
 
-    spare = jnp.logical_not(gate)
-    busy_inner = jnp.logical_and(inner, gate)
-    busy_end = jnp.logical_and(at_end, gate)
-    pl.when(inner)(lambda: carry_on(0))
     hear(place_of(0)[1])
-    pl.when(patient)(lambda: launch(0))
-    pl.when(outer_two)(lambda: launch(1))
     gather_entry(0)
+    carry_on(0)
 
     @pl.when(inner)
     def _():
-        gather_second(0)
+        gather_entry(1)
+        carry_on(1)
         gather(2)
-        gather(1)
-
-    @pl.when(at_end)
-    def _():
-        carry_on(0)
-        gather_second(1)
-
-    pl.when(later)(lambda: launch(1))
-    pl.when(outer_three)(lambda: launch(1))
-    pl.when(spare)(lambda: carry_on(1))
+
     whole_u.wait()
     rm_copy.wait()
     fronts.wait()
@@ -364,29 +385,17 @@
             send(v, a, l)
 
     def edge_gather(k):
+        if k < 5:
+            gather_entry(k + 1)
         if k == 0:
-            pl.when(busy_end)(lambda: carry_on(1))
-            gather_second(2)
-            gather_entry(1)
-            gather_entry(2)
-        if k == 1:
-            gather(3)
-        if k == 2:
-            gather_entry(4)
-        if k == 3:
-            gather_second(4)
-            gather(5)
+            carry_on(1)
+        if k == 5:
             gather_entry(6)
             gather_entry(7)
 
     def inner_gather(k):
-        if k == 0:
-            pl.when(busy_inner)(lambda: carry_on(1))
-            gather(3)
-        if k == 1:
-            gather(4)
-        if k == 2:
-            gather(5)
+        if k < 3:
+            gather(k + 3)
         if k == 3:
             gather_entry(6)
             gather_entry(7)
@@ -456,11 +465,15 @@
         copy.wait_send()
     for v in range(levels):
         way(v).wait_send()
-        pl.when(crosses[v])(cross(v).wait_send)
-        pl.when(helps[v])(onward(v).wait_send)
-        pl.when(away)(place(v, 0).wait_send)
-        if v == 0:
-            pl.when(direct)(place(v, 1).wait_send)
+        pl.when(distant)(deposit(v).wait_send)
+        for h in range(2):
+            pl.when(crosses[h])(cross(v, h).wait_send)
+            pl.when(helps[h])(onward(v, h).wait_send)
+            pending = jnp.logical_and(places[h], jnp.logical_not(distant))
+            if v == 1 and h == 0:
+                pending = jnp.logical_and(pending, jnp.logical_not(opener))
+            pl.when(late)(pick_up(v, h).wait_send)
+            pl.when(pending)(place(v, h).wait_send)
 
         def drain(a, carry, v=v):
             for h in range(2):
@@ -500,7 +513,7 @@
             pltpu.VMEM((levels, width, depth), bf16),
             pltpu.VMEM(upanel[:, 0].shape, bf16),
             pltpu.VMEM(front_blocks.shape, bf16),
-            pltpu.VMEM((levels, width // 2, depth), bf16),
+            pltpu.VMEM((levels, width, depth), bf16),
             pltpu.VMEM((levels, rows, width, depth), bf16),
             pltpu.VMEM((rows,) + blockmask.shape[:1] + blockmask.shape[2:], jnp.int32),
             pltpu.VMEM((levels, rows, layers, width, width), jnp.float32),
@@ -511,9 +524,9 @@
             pltpu.VMEM((1, 1, levels), jnp.int32),
             dma((7,)),
             dma((levels,)),
-            dma((levels,)),
-            dma((levels,)),
-            dma((levels,)),
+            dma((levels, 2)),
+            dma((levels, 2)),
+            dma((levels, 2)),
             dma((levels, 2)),
             dma((levels, 2, rows)),
             dma((levels, 2, rows)),
@@ -526,6 +539,11 @@
             dma((levels,)),
             dma,
             dma,
+            pltpu.SemaphoreType.REGULAR,
+            pltpu.VMEM((levels, width, depth), bf16),
+            dma((levels,)),
+            dma((levels,)),
+            dma((levels, 2)),
         ],
         compiler_params=pltpu.CompilerParams(collective_id=0, has_side_effects=True),
     )(

time: 56 us -> 54 us (0.964)
  Pallas kernels: 54 us -> 51.7 us
    pallas_call x1, Pallas kernels: 54 us -> 51.7 us  [stationary(): pl.pallas_call(functools.partial(kernel, rows, cols, layers, levels, widt...]
where the time goes in v4:
time: 54 us; the launch traced here: 53.6 us
  Pallas kernels  51.7 us (96%)
  local copies, waits for them, and re-layouts  1.87 us (3%)
    pallas_call x1, Pallas kernels, stationary(): pl.pallas_call(functools.partial(kernel, rows, cols, layers, levels, widt...  51.7 us
    unnamed x1, local copies, waits for them, and re-layouts  1.87 us

profile of v4, /device:TPU:0, one launch (start us, length us, event | category | flops | bytes accessed | tf_op | source)
XLA Modules:
  0.0 53.6 jit_solution(5002793317151068614)
XLA Ops:
  0.0 51.7 %shard_map.64 = bf16[2,512,256]{2,1,0:T(8,128)(2,1)} custom-call(bf16[2,256,512]{2,1,0:T(8,128)(2,1)} %bitcast.7, bf16[2,512,1024]{2,1,0:T(8,128)(2,1)} %bitcast.6, s32[2,1,4]{2,1,0:T(1,128)} %cm_hbm.1, s32[2,1,4]{2,1,0:T(1,128)} %bitcast.8, s32[1,1,2]{2,1,0:T(1,128)} %bitcast.9, bf16[2,512,256]{2,1,0:T(8,128)(2,1)} %front_hbm.1), custom_call_target="tpu_custom_call" | custom-call | tf_op jit(solution)/shard_map/pallas_call | solution.py:504
  51.7 1.9 %copy.9 = bf16[2,512,256]{2,1,0:T(8,128)(2,1)} copy(bf16[2,512,256]{2,1,0:T(8,128)(2,1)} %shard_map.64) | data formatting | bytes 1048576

commit v5 on v4

--- a/solution.py
+++ b/solution.py
@@ -375,8 +375,8 @@
         0: ((0, near, other),),
         1: ((1, near, other),),
         2: ((0, mid, other),),
-        3: ((0, end, other), (0, end, g)),
-        4: ((1, end, other), (1, end, g)),
+        3: ((0, end, other),),
+        4: ((1, end, other), (0, end, g), (1, end, g)),
         5: ((1, mid, other), (0, mid, g), (1, mid, g), (0, near, g), (1, near, g)),
     }
 
@@ -406,29 +406,71 @@
         if k in (1, 2):
             hear(place_of(k + 1)[1])
 
+    def hops_out(v):
+        for step in range(1, rows):
+            a = lax.rem(z + step, rows)
+            for l in range(layers):
+                hop(v, a, l, 0, a).wait_send()
+
+    def settle():
+        for copy in live_out:
+            copy.wait_send()
+        for v in range(levels):
+            pl.when(distant)(deposit(v).wait_send)
+            for h in range(2):
+                pl.when(crosses[h])(cross(v, h).wait_send)
+                pl.when(helps[h])(onward(v, h).wait_send)
+                pending = jnp.logical_and(places[h], jnp.logical_not(distant))
+                if v == 1 and h == 0:
+                    pending = jnp.logical_and(pending, jnp.logical_not(opener))
+                pl.when(late)(pick_up(v, h).wait_send)
+                pl.when(pending)(place(v, h).wait_send)
+
+        @pl.when(gate)
+        def _():
+            for v in range(levels):
+                def drain(a, carry, v=v):
+                    for h in range(2):
+                        post, relay = passes(v, a, h)
+                        relay.wait_send()
+                        there = turned(v, a, h)
+                        posted = jnp.logical_or(
+                            jnp.logical_and(entry, jnp.logical_not(there)),
+                            jnp.logical_and(second, there),
+                        )
+                        pl.when(posted)(post.wait_send)
+                    return carry
+
+                lax.fori_loop(0, rows, drain, 0)
+
+        for v in range(levels - 1):
+            way(v).wait_send()
+            hops_out(v)
+
     def inner_step(k):
         if k == 3:
             ahead(0, across_mid, other)
             ahead(0, far_end, other)
         if k == 5:
+            ahead(1, far_end, other)
             ahead(0, far_end, g)
-            ahead(1, far_end, other)
             back(0, other)
         if k == 6:
             collect(0, other, inward)
             collect(0, other, outward)
             trade(0)
             ahead(1, far_end, g)
-            back(0, g)
+            back(1, other)
         if k == 7:
             ahead(1, across_mid, other)
-            back(1, other)
+            back(0, g)
             ahead(0, across_mid, g)
             back(1, g)
             collect(1, other, inward)
             collect(1, other, outward)
             trade(1)
             ahead(1, across_mid, g)
+            settle()
             collect(0, g, outward)
             collect(0, g, inward)
             finish(0)
@@ -453,46 +495,16 @@
     def _():
         collect(0, other, outward)
         trade(0)
-        collect(0, g, outward)
         collect(1, other, outward)
         trade(1)
+        collect(0, g, outward)
+        settle()
         finish(0)
         collect(1, g, outward)
 
     finish(1)
-
-    for copy in live_out:
-        copy.wait_send()
-    for v in range(levels):
-        way(v).wait_send()
-        pl.when(distant)(deposit(v).wait_send)
-        for h in range(2):
-            pl.when(crosses[h])(cross(v, h).wait_send)
-            pl.when(helps[h])(onward(v, h).wait_send)
-            pending = jnp.logical_and(places[h], jnp.logical_not(distant))
-            if v == 1 and h == 0:
-                pending = jnp.logical_and(pending, jnp.logical_not(opener))
-            pl.when(late)(pick_up(v, h).wait_send)
-            pl.when(pending)(place(v, h).wait_send)
-
-        def drain(a, carry, v=v):
-            for h in range(2):
-                post, relay = passes(v, a, h)
-                pl.when(gate)(relay.wait_send)
-                there = turned(v, a, h)
-                posted = jnp.logical_or(
-                    jnp.logical_and(entry, jnp.logical_not(there)), jnp.logical_and(second, there)
-                )
-                pl.when(posted)(post.wait_send)
-
-            @pl.when(a != z)
-            def _():
-                for l in range(layers):
-                    hop(v, a, l, 0, z).wait_send()
-
-            return carry
-
-        lax.fori_loop(0, rows, drain, 0)
+    hops_out(levels - 1)
+    way(levels - 1).wait_send()
 
 
 def stationary(rows, cols, layers, lpanel, upanel, rowmap, colmap, blockmask, front_blocks):
@@ -503,7 +515,7 @@
     dma = pltpu.SemaphoreType.DMA
     return pl.pallas_call(
         functools.partial(kernel, rows, cols, layers, levels, width),
-        out_shape=jax.ShapeDtypeStruct(front_blocks.shape, front_blocks.dtype),
+        out_shape=pltpu.VMEM(front_blocks.shape, front_blocks.dtype),
         in_specs=[hbm] * 6,
         out_specs=vmem,
         scratch_shapes=[

time: 54 us -> 51.8 us (0.959)
  the two profiles are of different devices: /device:TPU:0 before, /device:TPU:11 now
where the time goes in v5:
time: 51.8 us; the launch traced here: 51.7 us
  Pallas kernels  50.9 us (98%)
  local copies, waits for them, and re-layouts  0.8 us (2%)
    pallas_call x1, Pallas kernels, stationary(): pl.pallas_call(functools.partial(kernel, rows, cols, layers, levels, widt...  50.9 us

profile of v5, /device:TPU:11, one launch (start us, length us, event | category | flops | bytes accessed | tf_op | source)
XLA Modules:
  0.0 51.7 jit_solution(14009156847653769288)
XLA Ops:
  0.0 50.9 %shard_map.64 = bf16[2,512,256]{2,1,0:T(8,128)(2,1)S(1)} custom-call(bf16[2,256,512]{2,1,0:T(8,128)(2,1)} %bitcast.7, bf16[2,512,1024]{2,1,0:T(8,128)(2,1)} %bitcast.6, s32[2,1,4]{2,1,0:T(1,128)} %cm_hbm.1, s32[2,1,4]{2,1,0:T(1,128)} %bitcast.8, s32[1,1,2]{2,1,0:T(1,128)} %bitcast.9, bf16[2,512,256]{2,1,0:T(8,128)(2,1)} %front_hbm.1), custom_call_target="tpu_custom_call" | custom-call | tf_op jit(solution)/shard_map/pallas_call | solution.py:516
  50.9 0.8 %copy.9 = bf16[2,512,256]{2,1,0:T(8,128)(2,1)} copy(bf16[2,512,256]{2,1,0:T(8,128)(2,1)S(1)} %shard_map.64) | data formatting | bytes 1048576

commit v6 on v5

--- a/solution.py
+++ b/solution.py
@@ -55,11 +55,10 @@
 def kernel(
     rows, cols, layers, levels, width,
     l_hbm, u_hbm, cm_hbm, live_hbm, rm_hbm, front_hbm, out_ref,
-    cm_ref, live_ref, rm_ref,
-    l_ref, u_ref, front_ref, crossed, l_all, live_all, own, part, p_in, y_out, y_in, rm_in,
-    in_sem, own_sem, x_send, x_recv, c_send, l_send, l_recv, post_send, relay_send,
-    m_send, m_recv, p_send, p_recv, y_send, y_recv, rm_send, rm_recv,
-    turn, stash, f_send, f_recv, g_send,
+    cm_ref, rm_ref,
+    l_ref, u_ref, front_ref, crossed, stash, l_all, live_all, own, part, p_in, y_out, y_in, rm_in,
+    in_sem, own_sem, x_recv, c_send, l_send, l_recv, post_send, relay_send,
+    m_send, m_recv, p_send, p_recv, y_send, y_recv, rm_send, rm_recv, turn, f_recv, g_send,
 ):
     z = lax.axis_index("row")
     c = lax.axis_index("col")
@@ -95,7 +94,7 @@
     small = [
         pltpu.make_async_copy(src, dst, in_sem.at[3 + i])
         for i, (src, dst) in enumerate(
-            ((live_hbm, live_ref), (rm_hbm, rm_ref), (cm_hbm, cm_ref), (live_hbm, live_all.at[z]))
+            ((live_hbm, live_all.at[z]), (rm_hbm, rm_ref), (cm_hbm, cm_ref))
         )
     ]
     for copy in small:
@@ -105,13 +104,8 @@
     fronts = pltpu.make_async_copy(front_hbm, front_ref, in_sem.at[2])
     fronts.start()
 
-    def own_load(v):
-        return pltpu.make_async_copy(l_hbm.at[v], l_all.at[v, z], own_sem.at[v])
-
-    @pl.when(entry)
-    def _():
-        for v in range(levels):
-            own_load(v).start()
+    own_load = pltpu.make_async_copy(l_hbm, l_all.at[:, z], own_sem)
+    pl.when(entry)(own_load.start)
 
     for copy in small:
         copy.wait()
@@ -124,19 +118,19 @@
     def place(v, h):
         return remote(
             l_ref.at[v, pieces[h]], l_all.at[v, z, pieces[h]],
-            l_send.at[v, h], l_recv.at[v, h, z], {"row": c},
+            l_send.at[v * (1 - h)], l_recv.at[v, h, z], {"row": c},
         )
 
     def cross(v, h):
         return remote(
             l_ref.at[v, pieces[h]], crossed.at[v, pieces[h]],
-            x_send.at[v, h], x_recv.at[v, h], {"col": far},
+            l_send.at[v * (1 - h)], x_recv.at[v, h], {"col": far},
         )
 
     def onward(v, h):
         return remote(
             crossed.at[v, pieces[h]], l_all.at[v, z, pieces[h]],
-            c_send.at[v, h], l_recv.at[v, h, z], {"row": far},
+            c_send, l_recv.at[v, h, z], {"row": far},
         )
 
     def routes(q):
@@ -164,9 +158,7 @@
     live_out = []
     for step in range(1, rows):
         to = lax.rem(z + step, rows)
-        live_out.append(
-            remote(live_ref, live_all.at[z], m_send.at[step], m_recv.at[z], {"row": to})
-        )
+        live_out.append(remote(live_all.at[z], live_all.at[z], m_send, m_recv, {"row": to}))
         live_out[-1].start()
     rm_copy = remote(rm_ref, rm_in, rm_send, rm_recv, {"gz": other})
     rm_copy.start()
@@ -181,12 +173,12 @@
     next_in = low + (1 - low) * (last - 1)
 
     def deposit(v):
-        return remote(l_ref.at[v], stash.at[v], f_send.at[v], f_recv.at[v], {"row": next_in})
+        return remote(l_ref.at[v], stash.at[v], l_send.at[0], f_recv.at[v], {"row": next_in})
 
     def pick_up(v, h):
         return remote(
             stash.at[v, pieces[h]], l_all.at[v, near_end, pieces[h]],
-            g_send.at[v, h], l_recv.at[v, h, near_end], {"row": c},
+            g_send, l_recv.at[v, h, near_end], {"row": c},
         )
 
     @pl.when(distant)
@@ -216,8 +208,8 @@
 
     def passes(v, a, h):
         spot = l_all.at[v, a, pieces[h]]
-        post = remote(spot, spot, post_send.at[v, h, a], l_recv.at[v, h, a], {"col": far})
-        relay = remote(spot, spot, relay_send.at[v, h, a], l_recv.at[v, h, a], {"col": mate})
+        post = remote(spot, spot, post_send.at[h], l_recv.at[v, h, a], {"col": far})
+        relay = remote(spot, spot, relay_send, l_recv.at[v, h, a], {"col": mate})
         return post, relay
 
     count = rows - 1
@@ -248,7 +240,8 @@
 
         @pl.when(entry)
         def _():
-            pl.when(a == z)(lambda: own_load(v).wait())
+            if k == levels * count:
+                own_load.wait()
             for h in range(2):
                 @pl.when(jnp.logical_not(turned(v, a, h)))
                 def _(h=h):
@@ -287,10 +280,10 @@
             for h in range(2):
                 passes(v, a, h)[1].wait_recv()
 
-    def hop(v, a, l, side, to):
+    def hop(v, a, l, side, row, to):
+        slot = a + (rows - a) * side * (a == row).astype(jnp.int32)
         return remote(
-            part.at[v, a, l], p_in.at[v, side, a, l],
-            p_send.at[v, a, l], p_recv.at[v, side, a, l], {"row": to},
+            part.at[v, a, l], p_in.at[v, slot, l], p_send, p_recv.at[v, slot, l], {"row": to}
         )
 
     inward, outward = 1 - low, low
@@ -298,7 +291,7 @@
 
     def send(v, a, l):
         part[v, a, l] = own[v, a, l].astype(jnp.bfloat16)
-        hop(v, a, l, inward, next_in).start()
+        hop(v, a, l, inward, next_in, next_in).start()
 
     def item(k):
         v, a = place_of(k)
@@ -317,10 +310,6 @@
                     own[v, a, l] += t * m
 
 
-    def hear(src):
-        remote(live_ref, live_all.at[src], m_send.at[1], m_recv.at[src], {"row": src}).wait_recv()
-
-    hear(place_of(0)[1])
     gather_entry(0)
     carry_on(0)
 
@@ -330,21 +319,28 @@
         carry_on(1)
         gather(2)
 
+    def flush(ref, sem):
+        pltpu.make_async_copy(ref, ref, sem).wait()
+
+    flush(live_all.at[: rows - 1], m_recv)
     whole_u.wait()
     rm_copy.wait()
     fronts.wait()
 
+    def taken_in(v, a, l, side):
+        slot = a + (rows - a) * side * (a == z).astype(jnp.int32)
+        hop(v, a, l, side, z, z).wait_recv()
+        return p_in[v, slot, l].astype(jnp.float32)
+
     def collect(v, l, side):
-        hop(v, z, l, side, z).wait_recv()
-        own[v, z, l] += p_in[v, side, z, l].astype(jnp.float32)
+        own[v, z, l] += taken_in(v, z, l, side)
 
     def forward(v, a, l, side, to):
-        hop(v, a, l, side, to).wait_recv()
-        part[v, a, l] = (own[v, a, l] + p_in[v, side, a, l].astype(jnp.float32)).astype(jnp.bfloat16)
-        hop(v, a, l, side, to).start()
+        part[v, a, l] = (own[v, a, l] + taken_in(v, a, l, side)).astype(jnp.bfloat16)
+        hop(v, a, l, side, to, to).start()
 
     def way(v):
-        return remote(y_out.at[v], y_in.at[v], y_send.at[v], y_recv.at[v], {"gz": other})
+        return remote(y_out.at[v], y_in.at[v], y_send, y_recv.at[v], {"gz": other})
 
     def trade(v):
         y_out[v] = own[v, z, other].astype(jnp.bfloat16)
@@ -403,49 +399,37 @@
     def shared_step(k):
         pl.when(at_end)(lambda: edge_gather(k))
         pl.when(inner)(lambda: inner_gather(k))
-        if k in (1, 2):
-            hear(place_of(k + 1)[1])
-
-    def hops_out(v):
-        for step in range(1, rows):
-            a = lax.rem(z + step, rows)
-            for l in range(layers):
-                hop(v, a, l, 0, a).wait_send()
 
     def settle():
-        for copy in live_out:
-            copy.wait_send()
-        for v in range(levels):
-            pl.when(distant)(deposit(v).wait_send)
-            for h in range(2):
-                pl.when(crosses[h])(cross(v, h).wait_send)
-                pl.when(helps[h])(onward(v, h).wait_send)
-                pending = jnp.logical_and(places[h], jnp.logical_not(distant))
-                if v == 1 and h == 0:
-                    pending = jnp.logical_and(pending, jnp.logical_not(opener))
-                pl.when(late)(pick_up(v, h).wait_send)
-                pl.when(pending)(place(v, h).wait_send)
+        some = p_in.at[0]
+        flush(live_all.at[: rows - 1], m_send)
+        pl.when(distant)(lambda: flush(some.at[:2], l_send.at[0]))
+        pl.when(nearby)(lambda: flush(some.at[: rows - 1, 0], l_send.at[0]))
+        single = jnp.logical_and(nearby, jnp.logical_not(opener))
+        pl.when(single)(place(1, 0).wait_send)
+        pl.when(late)(lambda: flush(some.at[:2], g_send))
+        pl.when(helps[0])(lambda: flush(some.at[:2], c_send))
+        only = jnp.logical_and(helps[1], jnp.logical_not(helps[0]))
+        pl.when(only)(lambda: flush(some.at[0], c_send))
 
         @pl.when(gate)
         def _():
-            for v in range(levels):
-                def drain(a, carry, v=v):
-                    for h in range(2):
-                        post, relay = passes(v, a, h)
-                        relay.wait_send()
-                        there = turned(v, a, h)
-                        posted = jnp.logical_or(
-                            jnp.logical_and(entry, jnp.logical_not(there)),
-                            jnp.logical_and(second, there),
-                        )
-                        pl.when(posted)(post.wait_send)
-                    return carry
-
-                lax.fori_loop(0, rows, drain, 0)
-
-        for v in range(levels - 1):
-            way(v).wait_send()
-            hops_out(v)
+            flush(l_all, relay_send)
+
+            @pl.when(jnp.logical_and(at_end, entry))
+            def _():
+                for h in range(2):
+                    flush(some.at[:rows], post_send.at[h])
+
+            @pl.when(jnp.logical_and(inner, entry))
+            def _():
+                flush(some.at[:3], post_send.at[0])
+                flush(some.at[:2], post_send.at[1])
+
+            @pl.when(jnp.logical_and(inner, second))
+            def _():
+                flush(some.at[0], post_send.at[0])
+                flush(some.at[:2], post_send.at[1])
 
     def inner_step(k):
         if k == 3:
@@ -503,8 +487,8 @@
         collect(1, g, outward)
 
     finish(1)
-    hops_out(levels - 1)
-    way(levels - 1).wait_send()
+    flush(p_in.at[:, : rows - 1], p_send)
+    flush(y_out, y_send)
 
 
 def stationary(rows, cols, layers, lpanel, upanel, rowmap, colmap, blockmask, front_blocks):
@@ -520,42 +504,39 @@
         out_specs=vmem,
         scratch_shapes=[
             pltpu.VMEM(colmap.shape, jnp.int32),
-            pltpu.VMEM((levels,) + blockmask.shape[2:], jnp.int32),
             pltpu.VMEM((1, 1, levels), jnp.int32),
             pltpu.VMEM((levels, width, depth), bf16),
             pltpu.VMEM(upanel[:, 0].shape, bf16),
             pltpu.VMEM(front_blocks.shape, bf16),
             pltpu.VMEM((levels, width, depth), bf16),
+            pltpu.VMEM((levels, width, depth), bf16),
             pltpu.VMEM((levels, rows, width, depth), bf16),
             pltpu.VMEM((rows,) + blockmask.shape[:1] + blockmask.shape[2:], jnp.int32),
             pltpu.VMEM((levels, rows, layers, width, width), jnp.float32),
             pltpu.VMEM((levels, rows, layers, width, width), bf16),
-            pltpu.VMEM((levels, 2, rows, layers, width, width), bf16),
+            pltpu.VMEM((levels, rows + 1, layers, width, width), bf16),
             pltpu.VMEM((levels, width, width), bf16),
             pltpu.VMEM((levels, width, width), bf16),
             pltpu.VMEM((1, 1, levels), jnp.int32),
-            dma((7,)),
+            dma((6,)),
+            dma,
+            dma((levels, 2)),
+            dma,
+            dma((2,)),
+            dma((levels, 2, rows)),
+            dma((2,)),
+            dma,
+            dma,
+            dma,
+            dma,
+            dma((levels, rows + 1, layers)),
+            dma,
             dma((levels,)),
-            dma((levels, 2)),
-            dma((levels, 2)),
-            dma((levels, 2)),
-            dma((levels, 2)),
-            dma((levels, 2, rows)),
-            dma((levels, 2, rows)),
-            dma((levels, 2, rows)),
-            dma((rows,)),
-            dma((rows,)),
-            dma((levels, rows, layers)),
-            dma((levels, 2, rows, layers)),
+            dma,
+            dma,
+            pltpu.SemaphoreType.REGULAR,
             dma((levels,)),
-            dma((levels,)),
-            dma,
-            dma,
-            pltpu.SemaphoreType.REGULAR,
-            pltpu.VMEM((levels, width, depth), bf16),
-            dma((levels,)),
-            dma((levels,)),
-            dma((levels, 2)),
+            dma,
         ],
         compiler_params=pltpu.CompilerParams(collective_id=0, has_side_effects=True),
     )(

time: 51.8 us -> 51.1 us (0.986)
  Pallas kernels: 50.9 us -> 50.2 us
    pallas_call x1, Pallas kernels: 50.9 us -> 50.2 us  [stationary(): pl.pallas_call(functools.partial(kernel, rows, cols, layers, levels, widt...]
where the time goes in v6:
time: 51.1 us; the launch traced here: 51 us
  Pallas kernels  50.2 us (98%)
  local copies, waits for them, and re-layouts  0.8 us (2%)
    pallas_call x1, Pallas kernels, stationary(): pl.pallas_call(functools.partial(kernel, rows, cols, layers, levels, widt...  50.2 us

profile of v6, /device:TPU:11, one launch (start us, length us, event | category | flops | bytes accessed | tf_op | source)
XLA Modules:
  0.0 51.0 jit_solution(6932394679866260404)
XLA Ops:
  0.0 50.2 %shard_map.64 = bf16[2,512,256]{2,1,0:T(8,128)(2,1)S(1)} custom-call(bf16[2,256,512]{2,1,0:T(8,128)(2,1)} %bitcast.7, bf16[2,512,1024]{2,1,0:T(8,128)(2,1)} %bitcast.6, s32[2,1,4]{2,1,0:T(1,128)} %cm_hbm.1, s32[2,1,4]{2,1,0:T(1,128)} %bitcast.8, s32[1,1,2]{2,1,0:T(1,128)} %bitcast.9, bf16[2,512,256]{2,1,0:T(8,128)(2,1)} %front_hbm.1), custom_call_target="tpu_custom_call" | custom-call | tf_op jit(solution)/shard_map/pallas_call | solution.py:500
  50.2 0.8 %copy.9 = bf16[2,512,256]{2,1,0:T(8,128)(2,1)} copy(bf16[2,512,256]{2,1,0:T(8,128)(2,1)S(1)} %shard_map.64) | data formatting | bytes 1048576

commit v7 on v6

--- a/solution.py
+++ b/solution.py
@@ -112,18 +112,20 @@
     first.wait()
     pl.semaphore_wait(barrier, rows + 2)
 
-    half = width // 2
-    pieces = [slice(h * half, (h + 1) * half) for h in range(2)]
+    parts = 4
+    lines = width // parts
+    pieces = [slice(h * lines, (h + 1) * lines) for h in range(parts)]
+    halves = [slice(h * 2 * lines, (h + 1) * 2 * lines) for h in range(2)]
 
     def place(v, h):
         return remote(
             l_ref.at[v, pieces[h]], l_all.at[v, z, pieces[h]],
-            l_send.at[v * (1 - h)], l_recv.at[v, h, z], {"row": c},
+            l_send.at[int(v == 1 and h == 0)], l_recv.at[v, h, z], {"row": c},
         )
 
     def cross(v, h):
         return remote(
-            l_ref.at[v, pieces[h]], crossed.at[v, pieces[h]],
+            l_ref.at[v, halves[h]], crossed.at[v, halves[h]],
             l_send.at[v * (1 - h)], x_recv.at[v, h], {"col": far},
         )
 
@@ -145,15 +147,17 @@
 
     def launch(v):
         for h in range(2):
-            pl.when(places[h])(lambda h=h: place(v, h).start())
             pl.when(crosses[h])(lambda h=h: cross(v, h).start())
+        for h in range(parts):
+            pl.when(places[h // 2])(lambda h=h: place(v, h).start())
 
     def carry_on(v):
         for h in range(2):
             @pl.when(helps[h])
             def _(h=h):
                 cross(v, h).wait_recv()
-                onward(v, h).start()
+                for n in range(2):
+                    onward(v, 2 * h + n).start()
 
     live_out = []
     for step in range(1, rows):
@@ -202,13 +206,13 @@
         launch(0)
         for v in range(levels):
             deposit(v).wait_recv()
-            for h in range(2):
+            for h in range(parts):
                 pick_up(v, h).start()
         launch(1)
 
     def passes(v, a, h):
         spot = l_all.at[v, a, pieces[h]]
-        post = remote(spot, spot, post_send.at[h], l_recv.at[v, h, a], {"col": far})
+        post = remote(spot, spot, post_send.at[h // 2], l_recv.at[v, h, a], {"col": far})
         relay = remote(spot, spot, relay_send, l_recv.at[v, h, a], {"col": mate})
         return post, relay
 
@@ -228,7 +232,7 @@
 
     def turned(v, a, h):
         both = a == last - z
-        return jnp.logical_and(inner, both if h == 0 else jnp.logical_or(both, (a - z) * (a - z) == 4))
+        return jnp.logical_and(inner, both if h < 2 else jnp.logical_or(both, (a - z) * (a - z) == 4))
 
     def spread(v, a, h):
         post, relay = passes(v, a, h)
@@ -242,7 +246,7 @@
         def _():
             if k == levels * count:
                 own_load.wait()
-            for h in range(2):
+            for h in range(parts):
                 @pl.when(jnp.logical_not(turned(v, a, h)))
                 def _(h=h):
                     pl.when(a != z)(lambda: passes(v, a, h)[1].wait_recv())
@@ -250,7 +254,7 @@
 
     def gather_second(k):
         v, a = place_of(k)
-        for h in range(2):
+        for h in range(parts):
             @pl.when(jnp.logical_and(second, turned(v, a, h)))
             def _(h=h):
                 passes(v, a, h)[1].wait_recv()
@@ -268,7 +272,7 @@
             relay.wait_recv()
             relay.start()
 
-        for h in range(2):
+        for h in range(parts):
             there = turned(v, a, h)
             taken = jnp.logical_or(
                 jnp.logical_and(second, jnp.logical_not(there)), jnp.logical_and(entry, there)
@@ -277,7 +281,7 @@
 
         @pl.when(jnp.logical_not(gate))
         def _():
-            for h in range(2):
+            for h in range(parts):
                 passes(v, a, h)[1].wait_recv()
 
     def hop(v, a, l, side, row, to):
@@ -404,8 +408,12 @@
         some = p_in.at[0]
         flush(live_all.at[: rows - 1], m_send)
         pl.when(distant)(lambda: flush(some.at[:2], l_send.at[0]))
-        pl.when(nearby)(lambda: flush(some.at[: rows - 1, 0], l_send.at[0]))
-        single = jnp.logical_and(nearby, jnp.logical_not(opener))
+        count_a = jnp.logical_and(nearby, jnp.logical_not(crosses[0]))
+        count_b = jnp.logical_and(nearby, crosses[0])
+        pl.when(count_a)(lambda: flush(u_ref.at[0, : 7 * lines // 2], l_send.at[0]))
+        pl.when(count_b)(lambda: flush(some.at[: rows - 1, 0], l_send.at[0]))
+        pl.when(count_b)(lambda: flush(some.at[0, 0], l_send.at[1]))
+        single = jnp.logical_and(count_a, jnp.logical_not(opener))
         pl.when(single)(place(1, 0).wait_send)
         pl.when(late)(lambda: flush(some.at[:2], g_send))
         pl.when(helps[0])(lambda: flush(some.at[:2], c_send))
@@ -523,7 +531,7 @@
             dma((levels, 2)),
             dma,
             dma((2,)),
-            dma((levels, 2, rows)),
+            dma((levels, 4, rows)),
             dma((2,)),
             dma,
             dma,

time: 51.1 us -> 49.9 us (0.977)
  the two profiles are of different devices: /device:TPU:11 before, /device:TPU:0 now
where the time goes in v7:
time: 49.9 us; the launch traced here: 49.2 us
  Pallas kernels  48.4 us (97%)
  local copies, waits for them, and re-layouts  0.8 us (2%)
    pallas_call x1, Pallas kernels, stationary(): pl.pallas_call(functools.partial(kernel, rows, cols, layers, levels, widt...  48.4 us

profile of v7, /device:TPU:0, one launch (start us, length us, event | category | flops | bytes accessed | tf_op | source)
XLA Modules:
  0.0 49.2 jit_solution(11886318454234370913)
XLA Ops:
  0.0 48.4 %shard_map.64 = bf16[2,512,256]{2,1,0:T(8,128)(2,1)S(1)} custom-call(bf16[2,256,512]{2,1,0:T(8,128)(2,1)} %bitcast.7, bf16[2,512,1024]{2,1,0:T(8,128)(2,1)} %bitcast.6, s32[2,1,4]{2,1,0:T(1,128)} %cm_hbm.1, s32[2,1,4]{2,1,0:T(1,128)} %bitcast.8, s32[1,1,2]{2,1,0:T(1,128)} %bitcast.9, bf16[2,512,256]{2,1,0:T(8,128)(2,1)} %front_hbm.1), custom_call_target="tpu_custom_call" | custom-call | tf_op jit(solution)/shard_map/pallas_call | solution.py:508
  48.4 0.8 %copy.9 = bf16[2,512,256]{2,1,0:T(8,128)(2,1)} copy(bf16[2,512,256]{2,1,0:T(8,128)(2,1)S(1)} %shard_map.64) | data formatting | bytes 1048576

commit v8 on v7

--- a/solution.py
+++ b/solution.py
@@ -264,7 +264,7 @@
         gather_entry(k)
         gather_second(k)
 
-    def take(k):
+    def take(k, part_of):
         v, a = place_of(k)
 
         def hand(h):
@@ -272,7 +272,7 @@
             relay.wait_recv()
             relay.start()
 
-        for h in range(parts):
+        for h in part_of:
             there = turned(v, a, h)
             taken = jnp.logical_or(
                 jnp.logical_and(second, jnp.logical_not(there)), jnp.logical_and(entry, there)
@@ -281,7 +281,7 @@
 
         @pl.when(jnp.logical_not(gate))
         def _():
-            for h in range(parts):
+            for h in part_of:
                 passes(v, a, h)[1].wait_recv()
 
     def hop(v, a, l, side, row, to):
@@ -297,9 +297,9 @@
         part[v, a, l] = own[v, a, l].astype(jnp.bfloat16)
         hop(v, a, l, inward, next_in, next_in).start()
 
-    def item(k):
+    def item(k, lane):
         v, a = place_of(k)
-        block = l_all[v, a]
+        block = l_all[v, a, lane, :]
         to_layer = cm_ref[v]
         live = live_all[a, v]
         for j in range(CB):
@@ -309,10 +309,9 @@
             for l in range(layers):
                 m = jnp.where(to_layer[:, j : j + 1] == l, live[:, j : j + 1], 0).astype(jnp.float32)
                 if j == 0:
-                    own[v, a, l] = t * m
+                    own[v, a, l, lane, :] = t * m
                 else:
-                    own[v, a, l] += t * m
-
+                    own[v, a, l, lane, :] += t * m
 
     gather_entry(0)
     carry_on(0)
@@ -470,8 +469,9 @@
             collect(1, g, inward)
 
     def body(k, carry):
-        take(k)
-        item(k)
+        for h in range(2):
+            take(k, range(2 * h, 2 * h + 2))
+            item(k, halves[h])
         for step in range(levels * rows):
             @pl.when(k == step)
             def _(step=step):

time: 49.9 us -> 49.8 us (level)
  no operation moved by 1% of the time
where the time goes in v8:
time: 49.8 us; the launch traced here: 49.2 us
  Pallas kernels  48.3 us (97%)
  local copies, waits for them, and re-layouts  0.8 us (2%)
    pallas_call x1, Pallas kernels, stationary(): pl.pallas_call(functools.partial(kernel, rows, cols, layers, levels, widt...  48.3 us

profile of v8, /device:TPU:0, one launch (start us, length us, event | category | flops | bytes accessed | tf_op | source)
XLA Modules:
  0.0 49.2 jit_solution(4464027619501900601)
XLA Ops:
  0.0 48.3 %shard_map.64 = bf16[2,512,256]{2,1,0:T(8,128)(2,1)S(1)} custom-call(bf16[2,256,512]{2,1,0:T(8,128)(2,1)} %bitcast.7, bf16[2,512,1024]{2,1,0:T(8,128)(2,1)} %bitcast.6, s32[2,1,4]{2,1,0:T(1,128)} %cm_hbm.1, s32[2,1,4]{2,1,0:T(1,128)} %bitcast.8, s32[1,1,2]{2,1,0:T(1,128)} %bitcast.9, bf16[2,512,256]{2,1,0:T(8,128)(2,1)} %front_hbm.1), custom_call_target="tpu_custom_call" | custom-call | tf_op jit(solution)/shard_map/pallas_call | solution.py:508
  48.4 0.8 %copy.9 = bf16[2,512,256]{2,1,0:T(8,128)(2,1)} copy(bf16[2,512,256]{2,1,0:T(8,128)(2,1)S(1)} %shard_map.64) | data formatting | bytes 1048576

commit v9 on v8

--- a/solution.py
+++ b/solution.py
@@ -469,9 +469,11 @@
             collect(1, g, inward)
 
     def body(k, carry):
-        for h in range(2):
-            take(k, range(2 * h, 2 * h + 2))
-            item(k, halves[h])
+        take(k, range(2))
+        item(k, halves[0])
+        for h in range(2, parts):
+            take(k, range(h, h + 1))
+            item(k, pieces[h])
         for step in range(levels * rows):
             @pl.when(k == step)
             def _(step=step):

time: 49.8 us -> 50 us (level)
  no operation moved by 1% of the time
where the time goes in v9:
time: 50 us; the launch traced here: 49.2 us
  Pallas kernels  48.3 us (97%)
  local copies, waits for them, and re-layouts  0.8 us (2%)
    pallas_call x1, Pallas kernels, stationary(): pl.pallas_call(functools.partial(kernel, rows, cols, layers, levels, widt...  48.3 us

profile of v9, /device:TPU:0, one launch (start us, length us, event | category | flops | bytes accessed | tf_op | source)
XLA Modules:
  0.0 49.2 jit_solution(2948043572169819199)
XLA Ops:
  0.0 48.3 %shard_map.64 = bf16[2,512,256]{2,1,0:T(8,128)(2,1)S(1)} custom-call(bf16[2,256,512]{2,1,0:T(8,128)(2,1)} %bitcast.7, bf16[2,512,1024]{2,1,0:T(8,128)(2,1)} %bitcast.6, s32[2,1,4]{2,1,0:T(1,128)} %cm_hbm.1, s32[2,1,4]{2,1,0:T(1,128)} %bitcast.8, s32[1,1,2]{2,1,0:T(1,128)} %bitcast.9, bf16[2,512,256]{2,1,0:T(8,128)(2,1)} %front_hbm.1), custom_call_target="tpu_custom_call" | custom-call | tf_op jit(solution)/shard_map/pallas_call | solution.py:510
  48.4 0.8 %copy.9 = bf16[2,512,256]{2,1,0:T(8,128)(2,1)} copy(bf16[2,512,256]{2,1,0:T(8,128)(2,1)S(1)} %shard_map.64) | data formatting | bytes 1048576
